TPU v7x, 128 devices: a whole 4x4x4 slice. The times are simulated.
128 devices in a mesh: dp: 32 (over z, y, x_hi), blk: 4 (over x_lo, core).
Axes of the slice: x: 4 (x_hi: 2, x_lo: 2; x = x_hi * 2 + x_lo), y: 4, z: 4, core: 2. Of those that a mesh axis runs over, the one named last changes fastest.
Arguments:
- tokens: bfloat16 [16384, 4096], P(('dp', 'blk')), may hold values from -6 to 6
- gate_projection_weight: bfloat16 [4096, 7168], P(None, 'blk'), may hold values from -0.09375 to 0.09375
- up_projection_weight: bfloat16 [4096, 7168], P('dp', 'blk'), may hold values from -0.09375 to 0.09375
- down_projection_weight: bfloat16 [7168, 4096], P('blk', 'dp'), may hold values from -0.0625 to 0.0625
- router_projection_weight: bfloat16 [4096, 8], replicated, may hold values from -0.09375 to 0.09375
- adapter_down_factors: bfloat16 [4096, 128], replicated, may hold values from -0.09375 to 0.09375
- adapter_up_factors: bfloat16 [128, 4096], replicated, may hold values from -1.5 to 1.5
- routes: int32 [16384, 2], P(('dp', 'blk')), may hold values from 0 to 7, all different within a row
- padding_token_mask: int32 [16384], P(('dp', 'blk')), may hold values 0 or 1
- cotangent: bfloat16 [16384, 4096], P(('dp', 'blk')), may hold values from -6 to 6
Outputs:
- layer_out: bfloat16 [16384, 4096], P(('dp', 'blk'))
- grad_down: float32 [4096, 128], replicated
- grad_up: float32 [128, 4096], replicated
Inputs may be any that keep to these rules, and one draw needn't show every extreme that they name: `routes`: the two experts of a token differ.
All inputs are finite; a program needn't handle non-finite values. No bound on the sum of `padding_token_mask` on one device may be relied on, other than what follows from the above.
Results may differ from a plain program's by a relative error of at most 0.0075.
Values may be sent and summed in bfloat16 or wider, within the bound.
A program may use at most 192 MiB of HBM per device.

v0:
```python
import jax
import jax.numpy as jnp
from jax import lax
from jax.sharding import PartitionSpec as P


def shards(
    tokens,
    gate_projection_weight,
    up_projection_weight,
    down_projection_weight,
    router_projection_weight,
    adapter_down_factors,
    adapter_up_factors,
    routes,
    padding_token_mask,
    cotangent,
):
    grouped = lax.all_gather(tokens, "blk", axis=0, tiled=True)
    gate_act = jnp.dot(grouped, gate_projection_weight, preferred_element_type=jnp.float32)
    up_act = jnp.dot(
        grouped,
        lax.all_gather(up_projection_weight, "dp", axis=0, tiled=True),
        preferred_element_type=jnp.float32,
    )
    down_full = lax.all_gather(down_projection_weight, "dp", axis=1, tiled=True)
    hidden = (jax.nn.silu(gate_act) * up_act).astype(jnp.bfloat16)
    part = jnp.dot(hidden, down_full, preferred_element_type=jnp.float32)
    part = lax.optimization_barrier(part.astype(jnp.bfloat16))
    base = lax.psum_scatter(
        part.astype(jnp.float32).astype(jnp.bfloat16), "blk", scatter_dimension=0, tiled=True
    ).astype(jnp.float32)
    expert_list = router_projection_weight.shape[1]
    rank_index = adapter_down_factors.shape[1] // expert_list
    logits = jnp.dot(tokens, router_projection_weight, preferred_element_type=jnp.float32)
    experts_iota = jnp.arange(expert_list, dtype=jnp.int32)[None, :]
    first_hot = (routes[:, 0:1] == experts_iota).astype(jnp.float32)
    second_hot = (routes[:, 1:2] == experts_iota).astype(jnp.float32)
    first_logit = jnp.sum(logits * first_hot, axis=1, keepdims=True)
    second_logit = jnp.sum(logits * second_hot, axis=1, keepdims=True)
    weight_first = jax.nn.sigmoid(first_logit - second_logit)
    coeff = weight_first * first_hot + (1.0 - weight_first) * second_hot
    coeff_wide = jnp.repeat(coeff, rank_index, axis=1)
    low_rank_state = jnp.dot(tokens, adapter_down_factors, preferred_element_type=jnp.float32)
    scaled_output = (low_rank_state * coeff_wide).astype(jnp.bfloat16)
    adapter_delta = jnp.dot(scaled_output, adapter_up_factors, preferred_element_type=jnp.float32)
    layer_out = (base + adapter_delta).astype(jnp.bfloat16)
    masked_tokens = cotangent * padding_token_mask[:, None].astype(jnp.bfloat16)
    low_rank_gradient = lax.dot_general(
        masked_tokens,
        adapter_up_factors,
        (((1,), (1,)), ((), ())),
        preferred_element_type=jnp.float32,
    )
    dlow = (low_rank_gradient * coeff_wide).astype(jnp.bfloat16)
    local_live = jnp.sum(padding_token_mask.astype(jnp.float32))
    local_up = lax.dot_general(
        scaled_output, masked_tokens, (((0,), (0,)), ((), ())), preferred_element_type=jnp.float32
    )
    local_down = lax.dot_general(
        tokens, dlow, (((0,), (0,)), ((), ())), preferred_element_type=jnp.float32
    )
    summed_down, summed_up, live_total = lax.psum((local_down, local_up, local_live), ("dp", "blk"))
    inverse = 1.0 / jnp.maximum(live_total, 1.0)
    grad_down = summed_down * inverse
    grad_up = summed_up * inverse
    return (layer_out, grad_down, grad_up)


def solution(mesh):
    return jax.shard_map(
        shards,
        mesh=mesh,
        in_specs=(
            P(("dp", "blk"), None),
            P(None, "blk"),
            P("dp", "blk"),
            P("blk", "dp"),
            P(),
            P(),
            P(),
            P(("dp", "blk"), None),
            P(("dp", "blk")),
            P(("dp", "blk"), None),
        ),
        out_specs=(P(("dp", "blk"), None), P(), P()),
        check_vma=False,
    )
```

profile of v0, /device:TPU:0, one launch (start us, length us, event | category | flops | bytes accessed | tf_op | source)
XLA Modules:
  0.0 509.0 jit_solution(5876728564059968191)
XLA Ops:
  8.0 0.0 copy-start
  8.0 0.0 copy-start.2
  8.0 0.0 all-gather.4.cloned.1.call-start
  8.1 0.7 all-gather.4.cloned.1.call-update
  8.8 0.0 all-gather.8.cloned.1.call-start
  8.8 0.7 all-gather.8.cloned.1.call-update
  9.5 0.0 copy-start.1
  9.5 0.0 all-gather.6.cloned.1.call-start
  9.6 0.7 all-gather.6.cloned.1.call-update
  10.3 0.0 all-reduce.3.cloned.1.call-start
  10.3 0.8 slice_bitcast_fusion.1
  11.1 1.6 select_reduce_fusion
  12.7 0.1 copy.15
  12.8 0.7 convert_element_type.34
  13.5 2.0 fusion.2
  15.5 0.0 copy-done.2
  15.5 1.8 fusion.4
  17.3 0.0 copy-done
  17.3 0.0 copy-done.1
  17.3 2.7 convolution_bitcast_fusion
  20.0 0.0 all-reduce.3.cloned.1.call-update
  20.0 0.2 reduce-scatter.2.cloned.1.call-start
  20.3 38.6 %all-gather.4.cloned.1.call-done = bf16[512,4096]{1,0:T(8,128)(2,1)} async-done(((bf16[128,4096]{1,0:T(8,128)(2,1)}), bf16[512,4096]{1,0:T(8,128)(2,1)}) %all-gather.4.cloned.1.call-update) | async-done | bytes 4194320 | tf_op jit(solution)/shard_map/all_gather | solution.py:19
  58.8 14.5 %fusion.12 = f32[512,1792]{1,0:T(8,128)} fusion(bf16[512,4096]{1,0:T(8,128)(2,1)} %all-gather.4.cloned.1.call-done, bf16[4096,1792]{1,0:T(8,128)(2,1)} %param.11), kind=kOutput, calls=%fused_computation.28 | convolution fusion | flops 7516192768 | bytes 22544384 | tf_op jit(solution)/shard_map/dot_general | solution.py:20
  73.3 180.0 %all-gather.8.cloned.1.call-done = bf16[1792,4096]{1,0:T(8,128)(2,1)} async-done(((bf16[1792,128]{1,0:T(8,128)(2,1)}), bf16[1792,4096]{1,0:T(8,128)(2,1)}) %all-gather.8.cloned.1.call-update) | async-done | bytes 14680080 | tf_op jit(solution)/shard_map/all_gather | solution.py:26
  253.3 145.3 %all-gather.6.cloned.1.call-done = bf16[4096,1792]{1,0:T(8,128)(2,1)} async-done(((bf16[128,1792]{1,0:T(8,128)(2,1)}), bf16[4096,1792]{1,0:T(8,128)(2,1)}) %all-gather.6.cloned.1.call-update) | async-done | bytes 14680080 | tf_op jit(solution)/shard_map/all_gather | solution.py:23
  398.6 28.6 %convolution_convert_fusion = bf16[512,4096]{1,0:T(8,128)(2,1)} fusion(bf16[1792,4096]{1,0:T(8,128)(2,1)} %all-gather.8.cloned.1.call-done, f32[512,1792]{1,0:T(8,128)} %fusion.12, bf16[512,4096]{1,0:T(8,128)(2,1)} %all-gather.4.cloned.1.call-done, bf16[4096,1792]{1,0:T(8,128)(2,1)} %all-gather.6.cloned.1.call-done), kind=kOutput, calls=%fused_computation | convolution fusion | flops 15039987712 | bytes 41418752 | tf_op jit(solution)/shard_map/dot_general | solution.py:28
  427.2 0.0 copy-start.3
  427.2 0.0 reduce-scatter.2.cloned.1.call-update
  427.2 0.6 copy-done.3
  427.8 0.6 convert_reduce_fusion
  428.4 63.4 %psum.22 = f32[]{:T(128)} all-reduce(f32[]{:T(128)} %convert_reduce_fusion), channel_id=1, replica_groups=mesh['dp'=32,'blk'=4] {'dp','blk'}, use_global_device_ids=true, to_apply=%region_5.6 | all-reduce | flops 1 | bytes 8 | tf_op jit(solution)/shard_map/psum | solution.py:63
  492.6 0.0 all-reduce.3.cloned.1.call-done
  492.6 1.8 broadcast_multiply_fusion.1
  494.4 1.8 copy.16
  496.2 3.1 broadcast_multiply_fusion
  499.3 0.0 reduce-scatter.2.cloned.1.call-done
  499.3 2.6 fusion
  (3 shorter events, 0.0 us)
Async XLA Ops:
  8.0 9.3 %copy-start = (bf16[128,4096]{1,0:T(8,128)(2,1)S(1)}, bf16[128,4096]{1,0:T(8,128)(2,1)}, u32[]{:S(2)}) copy-start(bf16[128,4096]{1,0:T(8,128)(2,1)} %param.16) | copy-start | bytes 3145732
  8.0 7.4 %copy-start.2 = (bf16[128,4096]{1,0:T(8,128)(2,1)S(1)}, bf16[128,4096]{1,0:T(8,128)(2,1)}, u32[]{:S(2)}) copy-start(bf16[128,4096]{1,0:T(8,128)(2,1)} %param.19) | copy-start | bytes 3145732
  8.0 50.8 %all-gather.4.cloned.1.call-start = ((), (), s32[]{:S(2)}) async-start(), calls=%async_computation.1 | async-start | bytes 5242880 | tf_op jit(solution)/shard_map/all_gather | solution.py:19
  8.8 244.6 %all-gather.8.cloned.1.call-start = ((), (), s32[]{:S(2)}) async-start(), calls=%async_computation.3 | async-start | bytes 15138816 | tf_op jit(solution)/shard_map/all_gather | solution.py:26
  9.5 7.8 %copy-start.1 = (bf16[128,4096]{1,0:T(8,128)(2,1)S(1)}, bf16[128,4096]{1,0:T(8,128)(2,1)}, u32[]{:S(2)}) copy-start(bf16[128,4096]{1,0:T(8,128)(2,1)} %param.10) | copy-start | bytes 3145732
  9.5 389.1 %all-gather.6.cloned.1.call-start = ((), (), s32[]{:S(2)}) async-start(), calls=%async_computation.2 | async-start | bytes 15138816 | tf_op jit(solution)/shard_map/all_gather | solution.py:23
  10.3 482.3 %all-reduce.3.cloned.1.call-start = ((), (), s32[]{:S(2)}) async-start(), calls=%async_computation.5 | async-start | bytes 8388608 | tf_op jit(solution)/shard_map/psum | solution.py:63
  20.0 479.3 %reduce-scatter.2.cloned.1.call-start = ((), (), s32[]{:S(2)}) async-start(), calls=%async_computation.4 | async-start | bytes 5242880 | tf_op jit(solution)/shard_map/reduce_scatter | solution.py:30
  427.2 0.7 copy-start.3
Sparse Core Ops, SparseCore 0:
  10.5 48.2 all-gather.3
  61.6 191.7 all-gather.7
  256.5 142.0 all-gather.5
  427.3 44.2 reduce-scatter.1
Sparse Core Ops, SparseCore 1:
  20.1 362.3 all-reduce.2
where the time goes:
time: 510 us; the launch traced here: 509 us
  waiting for transfers between devices  366 us (72%)
  blocking collectives  63.4 us (12%)
  matrix products  53.8 us (11%)
  between operations  16 us (3%)
  other arithmetic  6.15 us (1%)
    all_gather x1, waiting for transfers between devices, shards(): down_full = lax.all_gather(down_projection_weight, 'dp', axis=1, tiled=True)  180 us
    all_gather x1, waiting for transfers between devices, shards(): lax.all_gather(up_projection_weight, 'dp', axis=0, tiled=True)  145 us
    psum x1, blocking collectives, shards(): lax.psum((local_down, local_up, local_live), ('dp', 'blk'))  63.4 us
    all_gather x1, waiting for transfers between devices, shards(): grouped = lax.all_gather(tokens, 'blk', axis=0, tiled=True)  38.6 us
    dot_general x1, matrix products, shards(): part = jnp.dot(hidden, down_full, preferred_element_type=jnp.float32)  28.6 us
    dot_general x1, matrix products, shards(): jnp.dot(grouped, gate_projection_weight, preferred_element_type=jnp.float32)  14.5 us
  transfers between devices with their start and end apart: 5, of which 3 were waited for; matrix products, arithmetic and copies ran while one was open for 12% of the time, Pallas kernels for 0%

commit v1 on v0

v1 whole, which is shorter than its diff:
```python
import jax
import jax.numpy as jnp
from jax import lax
from jax.experimental import pallas as pl
from jax.experimental.pallas import tpu as pltpu
from jax.sharding import PartitionSpec as P

MESH = pl.DeviceIdType.MESH
BF, F32 = jnp.bfloat16, jnp.float32

REL = (0, 1, 3, 2)
LINK_RATE, PAIR_RATE = 46.6e3, 300e3
HOP, PAIR_HOP = 1.8, 1.0


class Copy:
    def __init__(self, name, link, size, source, landing, here, hops=1):
        self.name, self.link, self.size, self.hops = name, link, size, hops
        self.target = "xx" if hops == 2 else link
        self.source, self.landing, self.here = source, landing, here
        self.after = set()


class Task:
    def __init__(self, name, cost, run, after, rank):
        self.name, self.cost, self.run, self.after, self.rank = name, cost, run, set(after), rank


def arrange(copies, tasks, begun):
    order, done, now = [], set(begun), 0.0
    free, arriving = {}, []
    to_send, to_run = list(copies), list(tasks)

    def send_ready():
        for copy in list(to_send):
            if copy.after <= done:
                to_send.remove(copy)
                order.append(("send", copy))
                rate, hop = (PAIR_RATE, PAIR_HOP) if copy.link == "pair" else (LINK_RATE, HOP)
                start = max(now, free.get(copy.link, 0.0))
                end = start + copy.size * copy.hops / rate
                free[copy.link] = end
                arriving.append((end + hop * copy.hops, copy))

    send_ready()
    while arriving or to_run:
        arriving.sort(key=lambda pair: pair[0])
        ready = [task for task in to_run if task.after <= done]
        if arriving and arriving[0][0] <= now:
            copy = arriving.pop(0)[1]
            order.append(("recv", copy))
            done.add(copy.name)
            send_ready()
        elif ready:
            task = min(ready, key=lambda task: task.rank)
            to_run.remove(task)
            order.append(("task", task))
            now += task.cost
            done.add(task.name)
            send_ready()
        else:
            now = arriving[0][0]
    assert not to_send
    return order, now


def kernel(tokens, gate, up, down, base, tok, gw, ub, db, gact, uact, hid, psib, rsib, summed,
           rl, rr, fl, fr, load_sem, send_sem, recv_sem):
    dp, blk = lax.axis_index("dp"), lax.axis_index("blk")
    z, y, xh = dp // 8, (dp // 2) % 4, dp % 2
    xl, core = blk // 2, blk % 2
    x = xh * 2 + xl

    def device(dz=0, dy=0, dx=0, dc=0):
        at_z, at_y, at_x = (z + dz) % 4, (y + dy) % 4, (x + dx) % 4
        return ((at_z * 4 + at_y) * 2 + at_x // 2, (at_x % 2) * 2 + (core + dc) % 2)

    targets = {
        "z+": device(dz=1), "z-": device(dz=3), "y+": device(dy=1), "y-": device(dy=3),
        "x+": device(dx=1), "x-": device(dx=3), "xx": device(dx=2), "pair": device(dc=1),
    }

    def plane(dz, dy):
        return ((z + dz) % 4) * 4 + (y + dy) % 4

    copies = []

    def add(name, link, size, source, landing, here, after=(), hops=1):
        copy = Copy(name, link, size, source, landing, here, hops)
        copy.after = set(after)
        copies.append(copy)
        return copy

    piece = 128 * 896 * 2

    def weight(kind, dz, dy, own, half=None):
        ref, rows = (ub, 128) if kind == "u" else (db, 896)
        ref = ref.at[plane(dz, dy), xh if own else 1 - xh]
        if half is None:
            return ref
        return ref.at[pl.ds(half * (rows // 2), rows // 2)]

    def spread(kind, own, first, origin):
        tag = kind + ("o" if own else "p")
        second = "z" if first == "y" else "y"

        def at(f, s, half=None):
            dz, dy = (f, s) if first == "z" else (s, f)
            return weight(kind, dz, dy, own, half)

        def move(name, link, f, s, f_new, s_new, after, half=None):
            size = piece if half is None else piece // 2
            add(tag + name, link, size, at(f, s, half), at(f, s, half), at(f_new, s_new, half), after)

        move("F+", first + "+", 0, 0, 3, 0, [origin])
        move("F-", first + "-", 0, 0, 1, 0, [origin])
        move("S+0", second + "+", 0, 0, 0, 3, [origin])
        move("S-0", second + "-", 0, 0, 0, 1, [origin])
        move("G+", first + "+", 3, 0, 2, 0, [tag + "F+"], 0)
        move("G-", first + "-", 1, 0, 2, 0, [tag + "F-"], 1)
        came = {0: [origin], 3: [tag + "F+"], 1: [tag + "F-"], 2: [tag + "G+", tag + "G-"]}
        for f in REL[1:]:
            move("S+%d" % f, second + "+", f, 0, f, 3, came[f])
            move("S-%d" % f, second + "-", f, 0, f, 1, came[f])
        for f in (0, 1):
            move("T+%d" % f, second + "+", f, 3, f, 2, [tag + "S+%d" % f])
        for f in (3, 2):
            move("T-%d" % f, second + "-", f, 1, f, 2, [tag + "S-%d" % f])

        def have(f, s):
            if s == 0:
                return came[f]
            if s == 3:
                return [tag + "S+%d" % f]
            if s == 1:
                return [tag + "S-%d" % f]
            return [tag + ("T+%d" if f in (0, 1) else "T-%d") % f]

        return (lambda dz, dy: have(dz, dy)) if first == "z" else (lambda dz, dy: have(dy, dz))

    other = 1 - xh
    add("AU", "x+", piece, up.at[:, pl.ds(pl.multiple_of(other * 896, 128), 896)], ub.at[plane(0, 0), xh], ub.at[plane(0, 0), other], hops=2)
    mib = 128 * 4096 * 2
    add("K+", "x+", mib, tok.at[0, 0], tok.at[3, 0], tok.at[3, 0], ["L"])
    add("K-", "x-", mib, tok.at[0, 0], tok.at[1, 0], tok.at[1, 0], ["L"])
    add("KS0", "pair", mib, tok.at[0, 0], tok.at[0, 1], tok.at[0, 1], ["L"])
    add("AD", "x+", piece, down.at[pl.ds(pl.multiple_of(other * 896, 128), 896), :], db.at[plane(0, 0), xh], db.at[plane(0, 0), other], hops=2)
    have_uo = spread("u", True, "y", "L")
    have_up = spread("u", False, "z", "AU")
    have_do = spread("d", True, "z", "L")
    have_dp = spread("d", False, "y", "AD")
    low, high = pl.ds(0, 64), pl.ds(64, 64)
    add("KF+", "x+", mib // 2, tok.at[3, 0, low], tok.at[2, 0, low], tok.at[2, 0, low], ["K+"])
    add("KF-", "x-", mib // 2, tok.at[1, 0, high], tok.at[2, 0, high], tok.at[2, 0, high], ["K-"])
    add("KS3", "pair", mib, tok.at[3, 0], tok.at[3, 1], tok.at[3, 1], ["K+"])
    add("KS1", "pair", mib, tok.at[1, 0], tok.at[1, 1], tok.at[1, 1], ["K-"])
    add("KS2", "pair", mib, tok.at[2, 0], tok.at[2, 1], tok.at[2, 1], ["KF+", "KF-"])
    came_tok = {0: ["L", "KS0"], 3: ["K+", "KS3"], 1: ["K-", "KS1"], 2: ["KF+", "KF-", "KS2"]}

    tasks = []

    def project(r, weights, act, start):
        def step(i, carry):
            k = pl.multiple_of(i * 512, 512)
            left = tok[r, :, :, pl.ds(k, 512)].reshape(256, 512)
            part = jnp.dot(left, weights(i), preferred_element_type=F32)
            act[...] += part
            return carry

        act[...] = jnp.zeros_like(act)
        lax.fori_loop(0, 8, step, 0)

    def run_gate(r):
        def run():
            project(r, lambda i: gw[pl.ds(pl.multiple_of(i * 512, 512), 512), :], uact, 0)
            v = uact[...]
            gact[r] = v / (1.0 + jnp.exp(-v))
        return run

    def run_up(r):
        def run():
            project(r, lambda i: ub[pl.ds(i * 2, 2)].reshape(512, 896), uact, 0)
            hid[r] = (gact[r] * uact[...]).astype(BF)
        return run

    every_up = [n for dz in range(4) for dy in range(4) for n in have_uo(dz, dy) + have_up(dz, dy)]
    for rank, r in enumerate(REL):
        tasks.append(Task("G%d" % r, 2.6, run_gate(r), came_tok[r] + ["LG"], 10 + rank))
        tasks.append(Task("U%d" % r, 2.8, run_up(r), every_up + ["G%d" % r], 1 + rank))

    blocks = sorted(((dz, dy) for dz in range(4) for dy in range(4)), key=lambda p: (min(p[0], 4 - p[0]) + min(p[1], 4 - p[1]), p))
    size = 128 * 256 * 2

    def run_down(b, dz, dy):
        def run():
            j = plane(dz, dy)
            right = jnp.concatenate([db[j, 0], db[j, 1]], axis=1)

            def step(i, carry):
                left = hid[pl.ds(i * 2, 2)].reshape(512, 896)
                part = jnp.dot(left, right, preferred_element_type=F32).astype(BF).reshape(2, 2, 128, 256)
                summed[b, pl.ds(i * 2, 2)] = part[:, 0]
                psib[b, pl.ds(i * 2, 2)] = part[:, 1]
                return carry

            lax.fori_loop(0, 2, step, 0)
        return run

    def run_add(b):
        def run():
            summed[b] = (summed[b].astype(F32) + rsib[b].astype(F32)).astype(BF)
        return run

    def run_merge(b):
        def run():
            if b % 2 == 0:
                summed[b, 1] = (summed[b, 1].astype(F32) + rl[b // 2].astype(F32)).astype(BF)
            else:
                summed[b, 3] = (summed[b, 3].astype(F32) + rr[b // 2].astype(F32)).astype(BF)
        return run

    def run_final(b, dz, dy):
        def run():
            total = summed[b, 0].astype(F32) + fl[b].astype(F32) + fr[b].astype(F32)
            base[:, pl.ds(pl.multiple_of(plane(dz, dy) * 256, 256), 256)] = total
        return run

    hidden = ["U%d" % r for r in range(4)]
    for b, (dz, dy) in enumerate(blocks):
        n, half = str(b), b // 2
        tasks.append(Task("D" + n, 0.9, run_down(b, dz, dy), hidden + have_do(dz, dy) + have_dp(dz, dy), 300 + b))
        add("Q" + n, "pair", 4 * size, psib.at[b], rsib.at[b], rsib.at[b], ["D" + n])
        tasks.append(Task("A" + n, 0.15, run_add(b), ["D" + n, "Q" + n], 200 + b))
        if b % 2 == 0:
            add("Z" + n, "x+", size, summed.at[b, 2], rl.at[half], rl.at[half], ["A" + n])
            add("N" + n, "x-", size, summed.at[b, 3], fr.at[b], fr.at[b], ["A" + n])
            add("M" + n, "x+", size, summed.at[b, 1], fl.at[b], fl.at[b], ["C" + n])
        else:
            add("Z" + n, "x-", size, summed.at[b, 2], rr.at[half], rr.at[half], ["A" + n])
            add("N" + n, "x+", size, summed.at[b, 1], fl.at[b], fl.at[b], ["A" + n])
            add("M" + n, "x-", size, summed.at[b, 3], fr.at[b], fr.at[b], ["C" + n])
        tasks.append(Task("C" + n, 0.05, run_merge(b), ["A" + n, "Z" + n], 100 + b))
        tasks.append(Task("E" + n, 0.1, run_final(b, dz, dy), ["A" + n, "M" + n, "N" + n], 400 + b))

    order, _ = arrange(copies, tasks, ["L", "LG"])
    place = {copy.name: i for i, copy in enumerate(copies)}

    def descriptor(copy, landing):
        i = place[copy.name]
        return pltpu.make_async_remote_copy(
            src_ref=copy.source, dst_ref=landing, send_sem=send_sem.at[i], recv_sem=recv_sem.at[i],
            device_id=targets[copy.target], device_id_type=MESH)

    loads = [
        pltpu.make_async_copy(tokens, tok.at[0, 0], load_sem.at[0]),
        pltpu.make_async_copy(up.at[:, pl.ds(pl.multiple_of(xh * 896, 128), 896)], ub.at[plane(0, 0), xh], load_sem.at[1]),
        pltpu.make_async_copy(down.at[pl.ds(pl.multiple_of(xh * 896, 128), 896), :], db.at[plane(0, 0), xh], load_sem.at[2]),
    ]
    load_gate = pltpu.make_async_copy(gate.at[:, pl.ds(pl.multiple_of(xh * 896, 128), 896)], gw, load_sem.at[3])
    for load in loads:
        load.start()
    load_gate.start()
    barrier = pltpu.get_barrier_semaphore()
    for target in targets.values():
        pl.semaphore_signal(barrier, inc=1, device_id=target, device_id_type=MESH)
    pl.semaphore_wait(barrier, len(targets))
    for load in loads:
        load.wait()
    gate_waited = False
    for what, item in order:
        if what == "send":
            descriptor(item, item.landing).start()
        elif what == "recv":
            descriptor(item, item.here).wait_recv()
        else:
            if item.name[0] == "G" and not gate_waited:
                load_gate.wait()
                gate_waited = True
            item.run()
    for copy in copies:
        descriptor(copy, copy.landing).wait_send()


COPIES = 2 + 8 + 64 + 64


def frozen_block(tokens, gate, up, down):
    hbm = pl.BlockSpec(memory_space=pl.ANY)
    return pl.pallas_call(
        kernel,
        out_shape=jax.ShapeDtypeStruct((128, 4096), F32),
        in_specs=[hbm] * 4,
        out_specs=pl.BlockSpec(memory_space=pltpu.VMEM),
        scratch_shapes=[
            pltpu.VMEM((4, 2, 128, 4096), BF),
            pltpu.VMEM((4096, 896), BF),
            pltpu.VMEM((16, 2, 128, 896), BF),
            pltpu.VMEM((16, 2, 896, 128), BF),
            pltpu.VMEM((4, 256, 896), F32),
            pltpu.VMEM((256, 896), F32),
            pltpu.VMEM((4, 256, 896), BF),
            pltpu.VMEM((16, 4, 128, 256), BF),
            pltpu.VMEM((16, 4, 128, 256), BF),
            pltpu.VMEM((16, 4, 128, 256), BF),
            pltpu.VMEM((8, 128, 256), BF),
            pltpu.VMEM((8, 128, 256), BF),
            pltpu.VMEM((16, 128, 256), BF),
            pltpu.VMEM((16, 128, 256), BF),
            pltpu.SemaphoreType.DMA((4,)),
            pltpu.SemaphoreType.DMA((COPIES,)),
            pltpu.SemaphoreType.DMA((COPIES,)),
        ],
        compiler_params=pltpu.CompilerParams(
            collective_id=0, has_side_effects=True, vmem_limit_bytes=60 * 1024 * 1024),
        cost_estimate=pl.CostEstimate(flops=22_500_000_000, bytes_accessed=16_000_000, transcendentals=1_000_000),
        name="frozen_block",
    )(tokens, gate, up, down)


def shards(
    tokens,
    gate_projection_weight,
    up_projection_weight,
    down_projection_weight,
    router_projection_weight,
    adapter_down_factors,
    adapter_up_factors,
    routes,
    padding_token_mask,
    cotangent,
):
    expert_list = router_projection_weight.shape[1]
    rank_index = adapter_down_factors.shape[1] // expert_list
    logits = jnp.dot(tokens, router_projection_weight, preferred_element_type=F32)
    experts_iota = jnp.arange(expert_list, dtype=jnp.int32)[None, :]
    first_hot = (routes[:, 0:1] == experts_iota).astype(F32)
    second_hot = (routes[:, 1:2] == experts_iota).astype(F32)
    first_logit = jnp.sum(logits * first_hot, axis=1, keepdims=True)
    second_logit = jnp.sum(logits * second_hot, axis=1, keepdims=True)
    weight_first = jax.nn.sigmoid(first_logit - second_logit)
    coeff = weight_first * first_hot + (1.0 - weight_first) * second_hot
    coeff_wide = jnp.repeat(coeff, rank_index, axis=1)
    low_rank_state = jnp.dot(tokens, adapter_down_factors, preferred_element_type=F32)
    scaled_output = (low_rank_state * coeff_wide).astype(BF)
    masked_tokens = cotangent * padding_token_mask[:, None].astype(BF)
    low_rank_gradient = lax.dot_general(
        masked_tokens, adapter_up_factors, (((1,), (1,)), ((), ())), preferred_element_type=F32)
    dlow = (low_rank_gradient * coeff_wide).astype(BF)
    local_live = jnp.sum(padding_token_mask.astype(F32))
    local_up = lax.dot_general(
        scaled_output, masked_tokens, (((0,), (0,)), ((), ())), preferred_element_type=F32)
    local_down = lax.dot_general(
        dlow, tokens, (((0,), (0,)), ((), ())), preferred_element_type=F32)
    packed = jnp.concatenate([local_down, local_up, jnp.full((8, 4096), local_live, F32)], axis=0)
    packed = lax.psum(packed, ("dp", "blk"))
    base = frozen_block(tokens, gate_projection_weight, up_projection_weight, down_projection_weight)
    adapter_delta = jnp.dot(scaled_output, adapter_up_factors, preferred_element_type=F32)
    layer_out = (base + adapter_delta).astype(BF)
    inverse = 1.0 / jnp.maximum(packed[256, 0], 1.0)
    grad_down = packed[:128].T * inverse
    grad_up = packed[128:256] * inverse
    return (layer_out, grad_down, grad_up)


def solution(mesh):
    return jax.shard_map(
        shards,
        mesh=mesh,
        in_specs=(
            P(("dp", "blk"), None),
            P(None, "blk"),
            P("dp", "blk"),
            P("blk", "dp"),
            P(),
            P(),
            P(),
            P(("dp", "blk"), None),
            P(("dp", "blk")),
            P(("dp", "blk"), None),
        ),
        out_specs=(P(("dp", "blk"), None), P(), P()),
        check_vma=False,
    )
```

time: 510 us -> 201 us (0.39)
  waiting for transfers between devices: 366 us -> 0.96 us
  Pallas kernels: 0 us -> 160 us
  blocking collectives: 63.4 us -> 0 us
  matrix products: 53.8 us -> 9.78 us
    all_gather x3 -> x0, waiting for transfers between devices: 364 us -> none  [the longest x1 180 us: shards(): down_full = lax.all_gather(down_projection_weight, 'dp', axis=1, tiled=True)]
    pallas_call x0 -> x1, Pallas kernels: none -> 160 us  [frozen_block(): pl.pallas_call(kernel, out_shape=jax.ShapeDtypeStruct((128, 4096), F32),...]
    psum x1 -> x0, blocking collectives: 63.4 us -> none  [shards(): lax.psum((local_down, local_up, local_live), ('dp', 'blk'))]
    dot_general x6 -> x4, matrix products: 52 us -> 9.29 us  [the longest x1 3 us: shards(): jnp.dot(scaled_output, adapter_up_factors, preferred_element_type=F32)]
  transfers between devices with their start and end apart: 5 -> 1, of which waited for: 3 -> 1; matrix products, arithmetic and copies ran while one was open for 12% -> 2% of each run, Pallas kernels for 0% -> 80%
where the time goes in v1:
time: 201 us; the launch traced here: 199 us
  Pallas kernels  160 us (80%)
  between operations  14.8 us (7%)
  matrix products  9.78 us (5%)
  other arithmetic  8.59 us (4%)
  local copies, waits for them, and re-layouts  4.96 us (2%)
    pallas_call x1, Pallas kernels, frozen_block(): pl.pallas_call(kernel, out_shape=jax.ShapeDtypeStruct((128, 4096), F32),...  160 us
  transfers between devices with their start and end apart: 1, of which 1 were waited for; matrix products, arithmetic and copies ran while one was open for 2% of the time, Pallas kernels for 80%

profile of v1, /device:TPU:0, one launch (start us, length us, event | category | flops | bytes accessed | tf_op | source)
XLA Modules:
  0.0 199.3 jit_solution(981835492682568191)
XLA Ops:
  7.2 0.0 copy-start
  7.2 0.0 copy-start.1
  7.2 0.0 copy-start.3
  7.2 0.0 all-reduce.2.cloned.1.call-start
  7.2 1.4 convert_reduce_fusion
  8.7 0.7 convert_element_type.20
  9.3 0.8 slice_bitcast_fusion.1
  10.1 1.6 select_reduce_fusion
  11.7 0.1 copy.15
  11.8 2.0 fusion.2
  13.8 0.0 copy-done
  13.8 0.0 copy-done.1
  13.8 0.0 copy-done.3
  13.8 2.7 %fusion.4 = f32[128,4096]{1,0:T(8,128)} fusion(bf16[128,4096]{1,0:T(8,128)(2,1)S(1)} %copy-done.1, f32[128,128]{0,1:T(8,128)S(1)} %bitcast.18, bf16[128,4096]{1,0:T(8,128)(2,1)S(1)} %copy-done, bf16[128,4096]{1,0:T(8,128)(2,1)S(1)} %copy-done.3, bf16[128]{0:T(256)(128)(2,1)S(1)} %convert_element_type.20), kind=kOutput, calls=%fused_computation.10 | convolution fusion | flops 268992512 | bytes 5308672 | tf_op jit(solution)/shard_map/dot_general | solution.py:352
  16.6 0.0 copy-start.2
  16.6 0.5 fusion.5
  17.1 0.8 broadcast_in_dim.5
  17.9 0.3 copy-done.2
  18.1 2.6 %maximum_maximum_fusion = f32[264,4096]{1,0:T(8,128)} fusion(f32[128,4096]{1,0:T(8,128)S(1)} %fusion.5, f32[128,4096]{1,0:T(8,128)S(1)} %copy-done.2, f32[264]{0:T(512)S(1)} %pad.2.clone), kind=kLoop, calls=%fused_computation.2 | loop fusion | flops 2162688 | bytes 8520736 | tf_op jit(solution)/shard_map/concatenate | solution.py:354
  20.8 0.0 all-reduce.2.cloned.1.call-update
  20.8 160.1 %frozen_block.1 = f32[128,4096]{1,0:T(8,128)} custom-call(bf16[128,4096]{1,0:T(8,128)(2,1)} %tokens.1, bf16[4096,1792]{1,0:T(8,128)(2,1)} %gate.1, bf16[128,1792]{1,0:T(8,128)(2,1)} %up.1, bf16[1792,128]{1,0:T(8,128)(2,1)} %down.1), custom_call_target="tpu_custom_call" | custom-call | flops 22499999744 | bytes 16000000 | tf_op jit(solution)/shard_map/frozen_block/pallas_call | solution.py:289
  180.9 3.0 %fusion = bf16[128,4096]{1,0:T(8,128)(2,1)} fusion(f32[128,4096]{1,0:T(8,128)} %frozen_block.1, bf16[128,128]{1,0:T(8,128)(2,1)S(1)} %fusion.2, bf16[128,4096]{1,0:T(8,128)(2,1)S(1)} %copy-done), kind=kOutput, calls=%fused_computation.1 | convolution fusion | flops 135266304 | bytes 4227072 | tf_op jit(solution)/shard_map/dot_general | solution.py:357
  183.9 0.9 all-reduce.2.cloned.1.call-done
  184.8 1.2 slice.21
  186.7 3.9 %slice_multiply_fusion = (f32[128,4096]{1,0:T(8,128)}, f32[4096,128]{0,1:T(8,128)S(1)}) fusion(f32[264,4096]{1,0:T(8,128)} %all-reduce.2.cloned.1.call-done, f32[]{:T(128)} %bitcast.3), kind=kLoop, calls=%fused_computation.3 | loop fusion | flops 1048576 | bytes 8388612 | tf_op jit(solution)/shard_map/mul | solution.py:361
  190.6 1.8 copy.16
  (4 shorter events, 0.0 us)
Async XLA Ops:
  7.2 6.7 %copy-start = (bf16[128,4096]{1,0:T(8,128)(2,1)S(1)}, bf16[128,4096]{1,0:T(8,128)(2,1)}, u32[]{:S(2)}) copy-start(bf16[128,4096]{1,0:T(8,128)(2,1)} %param.16) | copy-start | bytes 3145732
  7.2 6.6 %copy-start.1 = (bf16[128,4096]{1,0:T(8,128)(2,1)S(1)}, bf16[128,4096]{1,0:T(8,128)(2,1)}, u32[]{:S(2)}) copy-start(bf16[128,4096]{1,0:T(8,128)(2,1)} %tokens.1) | copy-start | bytes 3145732
  7.2 6.6 %copy-start.3 = (bf16[128,4096]{1,0:T(8,128)(2,1)S(1)}, bf16[128,4096]{1,0:T(8,128)(2,1)}, u32[]{:S(2)}) copy-start(bf16[128,4096]{1,0:T(8,128)(2,1)} %param.19) | copy-start | bytes 3145732
  7.2 177.6 %all-reduce.2.cloned.1.call-start = ((), (), s32[]{:S(2)}) async-start(), calls=%async_computation | async-start | bytes 8650752 | tf_op jit(solution)/shard_map/psum | solution.py:355
  16.6 1.6 copy-start.2
Sparse Core Ops, SparseCore 0:
  20.9 163.8 all-reduce.1

commit v2 on v1

v2 whole, which is shorter than its diff:
```python
import jax
import jax.numpy as jnp
from jax import lax
from jax.experimental import pallas as pl
from jax.experimental.pallas import tpu as pltpu
from jax.sharding import PartitionSpec as P

MESH = pl.DeviceIdType.MESH
BF, F32 = jnp.bfloat16, jnp.float32

REL = (0, 1, 3, 2)
LINK_RATE, PAIR_RATE = 46.6e3, 300e3
HOP, PAIR_HOP = 1.8, 1.0
AHEAD = 1.5
GRAD_RANK = 50


class Copy:
    def __init__(self, name, link, size, source, landing, here, rank):
        self.name, self.link, self.size, self.rank = name, link, size, rank
        self.source, self.landing, self.here = source, landing, here
        self.after = set()


class Task:
    def __init__(self, name, cost, run, after, rank):
        self.name, self.cost, self.run, self.after, self.rank = name, cost, run, set(after), rank


def arrange(copies, tasks, begun):
    order, done, now = [], set(begun), 0.0
    free, arriving, queued = {}, [], {}
    to_send, to_run = list(copies), list(tasks)

    def send(copy):
        order.append(("send", copy))
        rate, hop = (PAIR_RATE, PAIR_HOP) if copy.link == "pair" else (LINK_RATE, HOP)
        start = max(now, free.get(copy.link, 0.0))
        free[copy.link] = end = start + copy.size / rate
        arriving.append((end + hop, copy))

    def send_ready(until):
        for copy in list(to_send):
            if copy.after <= done:
                to_send.remove(copy)
                queued.setdefault(copy.link, []).append(copy)
        for link, line in queued.items():
            line.sort(key=lambda copy: copy.rank)
            while line and (free.get(link, 0.0) < until or link == "pair"):
                send(line.pop(0))

    send_ready(AHEAD)
    while arriving or to_run:
        arriving.sort(key=lambda pair: pair[0])
        ready = [task for task in to_run if task.after <= done]
        if arriving and arriving[0][0] <= now:
            copy = arriving.pop(0)[1]
            order.append(("recv", copy))
            done.add(copy.name)
            send_ready(now + AHEAD)
        elif ready:
            task = min(ready, key=lambda task: task.rank)
            to_run.remove(task)
            order.append(("task", task))
            now += task.cost
            done.add(task.name)
            send_ready(now + AHEAD)
        else:
            send_ready(arriving[0][0] + AHEAD)
            arriving.sort(key=lambda pair: pair[0])
            now = arriving[0][0]
    assert not to_send
    return order, now


def kernel(tokens, gate, up, down, grad_low, grad_high, live, base, grads, tok, gw, ub, db, gact, uact, hid, psib, rsib, summed,
           rl, rr, fl, fr, ustage, dstage, g, own, live_pair, rz, rm, xs, ga, gb, load_sem, send_sem, recv_sem):
    dp, blk = lax.axis_index("dp"), lax.axis_index("blk")
    z, y, xh = dp // 8, (dp // 2) % 4, dp % 2
    xl, core = blk // 2, blk % 2
    x = xh * 2 + xl

    def device(dz=0, dy=0, dx=0, dc=0):
        at_z, at_y, at_x = (z + dz) % 4, (y + dy) % 4, (x + dx) % 4
        return ((at_z * 4 + at_y) * 2 + at_x // 2, (at_x % 2) * 2 + (core + dc) % 2)

    targets = {
        "z+": device(dz=1), "z-": device(dz=3), "y+": device(dy=1), "y-": device(dy=3),
        "x+": device(dx=1), "x-": device(dx=3), "pair": device(dc=1),
    }

    def plane(dz, dy):
        return ((z + dz) % 4) * 4 + (y + dy) % 4

    copies = []

    def add(name, link, size, source, landing, here, after=(), rank=0):
        copy = Copy(name, link, size, source, landing, here, rank)
        copy.after = set(after)
        copies.append(copy)
        return copy

    piece = 128 * 896 * 2

    def weight(kind, dz, dy, own, half=None):
        ref, rows = (ub, 128) if kind == "u" else (db, 896)
        ref = ref.at[plane(dz, dy), xh if own else 1 - xh]
        if half is None:
            return ref
        return ref.at[pl.ds(half * (rows // 2), rows // 2)]

    def spread(tag, ref, size, first, origin, base_rank):
        second = "z" if first == "y" else "y"

        def at(f, s, half=None):
            return ref(f, s, half) if first == "z" else ref(s, f, half)

        def move(name, link, f, s, f_new, s_new, after, rank, half=None):
            amount = size if half is None else size // 2
            add(tag + name, link, amount, at(f, s, half), at(f, s, half), at(f_new, s_new, half), after, rank + base_rank)

        move("F+", first + "+", 0, 0, 3, 0, origin, 0)
        move("F-", first + "-", 0, 0, 1, 0, origin, 0)
        move("S+0", second + "+", 0, 0, 0, 3, origin, 1)
        move("S-0", second + "-", 0, 0, 0, 1, origin, 1)
        move("G+", first + "+", 3, 0, 2, 0, [tag + "F+"], 2, 0)
        move("G-", first + "-", 1, 0, 2, 0, [tag + "F-"], 2, 1)
        came = {0: origin, 3: [tag + "F+"], 1: [tag + "F-"], 2: [tag + "G+", tag + "G-"]}
        for f in REL[1:]:
            move("S+%d" % f, second + "+", f, 0, f, 3, came[f], 4 if f == 2 else 3)
            move("S-%d" % f, second + "-", f, 0, f, 1, came[f], 4 if f == 2 else 3)
        for f in (0, 1):
            move("T+%d" % f, second + "+", f, 3, f, 2, [tag + "S+%d" % f], 5)
        for f in (3, 2):
            move("T-%d" % f, second + "-", f, 1, f, 2, [tag + "S-%d" % f], 5)

        def have(f, s):
            if s == 0:
                return came[f]
            if s == 3:
                return [tag + "S+%d" % f]
            if s == 1:
                return [tag + "S-%d" % f]
            return [tag + ("T+%d" if f in (0, 1) else "T-%d") % f]

        return (lambda dz, dy: have(dz, dy)) if first == "z" else (lambda dz, dy: have(dy, dz))

    def across(kind, hbm, ref, stage, rows, rank):
        for sign, step, half in (("+", 1, 0), ("-", 3, 1)):
            part = pl.ds(half * rows, rows)
            if kind == "u":
                source = hbm.at[part, pl.ds(pl.multiple_of((1 - xh) * 896, 128), 896)]
            else:
                source = hbm.at[pl.ds(pl.multiple_of((1 - xh) * 896 + half * rows, 64), rows), :]
            next_half = 1 - ((x + step) % 4) // 2
            hold = stage.at[half]
            add("A" + kind + sign, "x" + sign, piece // 2, source, hold, hold, [], rank)
            add("B" + kind + sign, "x" + sign, piece // 2, hold, ref.at[plane(0, 0), next_half, part],
                ref.at[plane(0, 0), 1 - xh, part], ["A" + kind + sign], rank)
        return ["B" + kind + "+", "B" + kind + "-"]

    mib = 128 * 4096 * 2
    have_au = across("u", up, ub, ustage, 64, 0)
    quarters = [pl.ds(32 * q, 32) for q in range(4)]
    for sign, r, order4 in (("+", 3, (0, 1, 2, 3)), ("-", 1, (2, 3, 0, 1))):
        for n, q in enumerate(order4):
            part = quarters[q]
            add("K%s%d" % (sign, q), "x" + sign, mib // 4, tok.at[0, 0, part], tok.at[r, 0, part], tok.at[r, 0, part], ["L", "Au" + sign], 3)
            if n < 2:
                add("KF%d" % q, "x" + sign, mib // 4, tok.at[r, 0, part], tok.at[2, 0, part], tok.at[2, 0, part], ["K%s%d" % (sign, q)], 4)
                add("KP%d" % q, "pair", mib // 4, tok.at[2, 0, part], tok.at[2, 1, part], tok.at[2, 1, part], ["KF%d" % q])
    came_near = {0: ["L"], 3: ["K+%d" % q for q in range(4)], 1: ["K-%d" % q for q in range(4)]}
    for r in (0, 1, 3):
        add("KS%d" % r, "pair", mib, tok.at[r, 0], tok.at[r, 1], tok.at[r, 1], came_near[r])
    came_near[2] = ["KF%d" % q for q in range(4)]
    came_pair = {r: ["KS%d" % r] for r in (0, 1, 3)}
    came_pair[2] = ["KP%d" % q for q in range(4)]
    have_ad = across("d", down, db, dstage, 448, 5)
    def piece_of(kind, own):
        return lambda dz, dy, half: weight(kind, dz, dy, own, half)

    have_uo = spread("uo", piece_of("u", True), piece, "y", ["L"], 0)
    have_up = spread("up", piece_of("u", False), piece, "z", have_au, 0)
    have_do = spread("do", piece_of("d", True), piece, "z", ["L"], 100)
    have_dp = spread("dp", piece_of("d", False), piece, "y", have_ad, 100)
    came_tok = {r: came_near[r] + came_pair[r] for r in REL}

    tasks = []

    def run_gate(places):
        def run():
            def step(i, carry):
                k = pl.multiple_of(i * 512, 512)
                left = jnp.concatenate([tok[r, :, :, pl.ds(k, 512)].reshape(256, 512) for r in places], axis=0)
                part = jnp.dot(left, gw[pl.ds(k, 512), :], preferred_element_type=F32)
                for n, r in enumerate(places):
                    uact[r] += part[n * 256:n * 256 + 256]
                return carry

            for r in places:
                uact[r] = jnp.zeros((256, 896), F32)
            lax.fori_loop(0, 8, step, 0)
            for r in places:
                v = uact[r]
                gact[r] = v / (1.0 + jnp.exp(-v))
                uact[r] = jnp.zeros((256, 896), F32)
        return run

    def run_up(dz, dy, i):
        def run():
            j = plane(dz, dy)
            columns = pl.ds(pl.multiple_of(j * 256, 256), 256)
            two = pl.ds(i * 2, 2)
            left = tok[two, :, :, columns].reshape(512, 256)
            part = jnp.dot(left, ub[j].reshape(256, 896), preferred_element_type=F32)
            uact[two] += part.reshape(2, 256, 896)
        return run

    def run_hidden():
        hid[...] = (gact[...] * uact[...]).astype(BF)

    ups = []
    for name, cost, places in (("G0", 5.7, (0,)), ("G1", 9.0, (1, 3)), ("G2", 5.7, (2,))):
        tasks.append(Task(name, cost, run_gate(places), [n for r in places for n in came_tok[r]] + ["LG"], 10))
    for dz in range(4):
        for dy in range(4):
            for i in (0, 1):
                ups.append("U%d%d%d" % (dz, dy, i))
                ready = have_uo(dz, dy) + have_up(dz, dy) + ["G1", "G2" if i else "G0"]
                tasks.append(Task(ups[-1], 0.45, run_up(dz, dy, i), ready, 20 + i))
    tasks.append(Task("H", 0.5, run_hidden, ups, 0))
    blocks = sorted(((dz, dy) for dz in range(4) for dy in range(4)), key=lambda p: (min(p[0], 4 - p[0]) + min(p[1], 4 - p[1]), p))
    size = 128 * 256 * 2

    slot = {}

    def run_down(b, dz, dy):
        def run():
            j = plane(dz, dy)
            right = jnp.concatenate([db[j, 0], db[j, 1]], axis=1)

            def step(i, carry):
                left = hid[pl.ds(i * 2, 2)].reshape(512, 896)
                part = jnp.dot(left, right, preferred_element_type=F32).astype(BF).reshape(2, 2, 128, 256)
                summed[b, pl.ds(i * 2, 2)] = part[:, 0]
                psib[slot[b], pl.ds(i * 2, 2)] = part[:, 1]
                return carry

            lax.fori_loop(0, 2, step, 0)
        return run

    def run_add(b):
        def run():
            summed[b] = (summed[b].astype(F32) + rsib[b].astype(F32)).astype(BF)
        return run

    def run_merge(b):
        def run():
            if b % 2 == 0:
                summed[b, 1] = (summed[b, 1].astype(F32) + rl[b // 2].astype(F32)).astype(BF)
            else:
                summed[b, 3] = (summed[b, 3].astype(F32) + rr[b // 2].astype(F32)).astype(BF)
        return run

    def run_final(b, dz, dy):
        def run():
            total = summed[b, 0].astype(F32) + fl[b].astype(F32) + fr[b].astype(F32)
            base[:, pl.ds(pl.multiple_of(plane(dz, dy) * 256, 256), 256)] = total
        return run

    hidden = ["H"]
    for b, (dz, dy) in enumerate(blocks):
        n, half = str(b), b // 2
        tasks.append(Task("D" + n, 1.25, run_down(b, dz, dy), hidden + have_do(dz, dy) + have_dp(dz, dy), 300 + b))
        add("Q" + n, "pair", 4 * size, None, rsib.at[b], rsib.at[b], ["D" + n])
        tasks.append(Task("A" + n, 0.15, run_add(b), ["D" + n, "Q" + n], 200 + b))
        if b % 2 == 0:
            add("Z" + n, "x+", size, summed.at[b, 2], rl.at[half], rl.at[half], ["A" + n], 10 + 3 * b)
            add("N" + n, "x-", size, summed.at[b, 3], fr.at[b], fr.at[b], ["A" + n], 12 + 3 * b)
            add("M" + n, "x+", size, summed.at[b, 1], fl.at[b], fl.at[b], ["C" + n], 11 + 3 * b)
        else:
            add("Z" + n, "x-", size, summed.at[b, 2], rr.at[half], rr.at[half], ["A" + n], 10 + 3 * b)
            add("N" + n, "x+", size, summed.at[b, 1], fl.at[b], fl.at[b], ["A" + n], 12 + 3 * b)
            add("M" + n, "x-", size, summed.at[b, 3], fr.at[b], fr.at[b], ["C" + n], 11 + 3 * b)
        tasks.append(Task("C" + n, 0.05, run_merge(b), ["A" + n, "Z" + n], 100 + b))
        tasks.append(Task("E" + n, 0.1, run_final(b, dz, dy), ["A" + n, "M" + n, "N" + n], 400 + b))

    wide = 1152 * 4
    pair_after = ["PL"]
    add("PL", "pair", 4096, live, live_pair, live_pair, [], 0)
    for ab in range(2):
        there = pl.ds(pl.multiple_of((1 - core) * 2048 + ab * 1024, 1024), 1024)
        for h, part in enumerate((grad_low, grad_high)):
            landing = g.at[ab, pl.ds(h * 128, 128), pl.ds(0, 1024)]
            add("PG%d%d" % (ab, h), "pair", 128 * 4096, part.at[:, there], landing, landing, [], 1)
            pair_after.append("PG%d%d" % (ab, h))

    def run_own():
        parts = [(ab, h, n) for ab in range(2) for h in range(2) for n in range(2)]

        def fetch(i):
            ab, h, n = parts[i]
            here = pl.ds(pl.multiple_of(core * 2048 + ab * 1024, 1024), 1024)
            part = (grad_low, grad_high)[h]
            return pltpu.make_async_copy(part.at[pl.ds(n * 64, 64), here], own.at[i % 2], load_sem.at[4 + i % 2])

        fetch(0).start()
        for i, (ab, h, n) in enumerate(parts):
            if i + 1 < len(parts):
                fetch(i + 1).start()
            fetch(i).wait()
            g[ab, h * 128 + n * 64:h * 128 + n * 64 + 64, 0:1024] += own[i % 2]
        count = live[0:1, :] + live_pair[0:1, :]
        for ab in range(2):
            g[ab, :, 1024:1152] = jnp.broadcast_to(count, (256, 128))

    tasks.append(Task("PA", 6.0, run_own, pair_after, 5))

    def reduce_ring(tag, axis, piece_at, hold_z, hold_m, rows, after, finish, rank):
        amount = rows * wide
        for sign, near, half in (("+", 1, 0), ("-", 3, 1)):
            add(tag + "Z" + sign, axis + sign, amount // 2, piece_at(2, half), hold_z.at[half], hold_z.at[half], after, rank)

            def combine(near=near, half=half):
                ref = piece_at(near, half)
                ref[...] = ref[...] + hold_z[half]

            tasks.append(Task(tag + "C" + sign, 0.2, combine, after + [tag + "Z" + sign], 6))
            add(tag + "M" + sign, axis + sign, amount, piece_at(near), hold_m.at[half], hold_m.at[half], [tag + "C" + sign], rank)
        tasks.append(Task(tag + "E", 0.3, finish, after + [tag + "M+", tag + "M-"], 6))

    row_of = {"y": y, "z": z}
    for ab, (first, second) in enumerate((("y", "z"), ("z", "y"))):
        p, q = row_of[first], row_of[second]

        def block(d, half=None, ab=ab, p=p):
            rows = pl.multiple_of(((p + d) % 4) * 64 + (half or 0) * 32, 32)
            return g.at[ab, pl.ds(rows, 64 if half is None else 32)]

        def small(d, half=None, ab=ab, p=p, q=q):
            rows = pl.multiple_of(p * 64 + ((q + d) % 4) * 16 + (half or 0) * 8, 8)
            return g.at[ab, pl.ds(rows, 16 if half is None else 8)]

        z1, m1 = rz.at[ab, :, pl.ds(0, 32)], rm.at[ab, :, pl.ds(0, 64)]
        z2, m2 = rz.at[ab, :, pl.ds(32, 8)], rm.at[ab, :, pl.ds(64, 16)]

        def first_done(block=block, ab=ab):
            ref = block(0)
            ref[...] = ref[...] + rm[ab, 0, 0:64] + rm[ab, 1, 0:64]

        def second_done(small=small, ab=ab):
            xs[0, ab] = small(0)[...] + rm[ab, 0, 64:80] + rm[ab, 1, 64:80]

        reduce_ring("R%d" % ab, first, block, z1, m1, 64, ["PA"], first_done, GRAD_RANK)
        reduce_ring("S%d" % ab, second, small, z2, m2, 16, ["R%dE" % ab], second_done, GRAD_RANK)

    slices = ["S0E", "S1E"]
    add("X+", "x+", 32 * wide, xs.at[0], xs.at[3], xs.at[3], slices, 6)
    add("X-", "x-", 32 * wide, xs.at[0], xs.at[1], xs.at[1], slices, 6)
    add("XF+", "x+", 16 * wide, xs.at[3, 0], xs.at[2, 0], xs.at[2, 0], ["X+"], 6)
    add("XF-", "x-", 16 * wide, xs.at[1, 1], xs.at[2, 1], xs.at[2, 1], ["X-"], 6)

    def row_block(ab, dz, dy):
        at_z, at_y = (z + dz) % 4, (y + dy) % 4
        return at_z * 4 + at_y if ab else at_y * 4 + at_z

    def run_whole():
        for ab in range(2):
            total = (xs[0, ab] + xs[2, ab]) + (xs[1, ab] + xs[3, ab])
            inverse = 1.0 / jnp.maximum(total[:, 1024:1025], 1.0)
            ga[ab, row_block(ab, 0, 0)] = (total[:, 0:1024] * inverse).astype(BF)

    tasks.append(Task("XS", 0.4, run_whole, slices + ["X+", "X-", "XF+", "XF-"], 6))
    for ab, first in enumerate("yz"):
        def finished(dz, dy, half, ab=ab):
            ref = ga.at[ab, row_block(ab, dz, dy)]
            return ref if half is None else ref.at[:, pl.ds(half * 512, 512)]

        have = spread("g%d" % ab, finished, 16 * 1024 * 2, first, ["XS"], GRAD_RANK)
        whole = sorted({n for dz in range(4) for dy in range(4) for n in have(dz, dy)})
        add("PH%d" % ab, "pair", 256 * 1024 * 2, ga.at[ab], gb.at[ab], gb.at[ab], whole)

    order, _ = arrange(copies, tasks, ["L", "LG"])
    assert len(copies) == COPIES
    place = {copy.name: i for i, copy in enumerate(copies)}
    by_name = {copy.name: copy for copy in copies}

    def descriptor(copy, landing):
        i = place[copy.name]
        return pltpu.make_async_remote_copy(
            src_ref=copy.source, dst_ref=landing, send_sem=send_sem.at[i], recv_sem=recv_sem.at[i],
            device_id=targets[copy.link], device_id_type=MESH)

    loads = [
        pltpu.make_async_copy(tokens, tok.at[0, 0], load_sem.at[0]),
        pltpu.make_async_copy(up.at[:, pl.ds(pl.multiple_of(xh * 896, 128), 896)], ub.at[plane(0, 0), xh], load_sem.at[1]),
        pltpu.make_async_copy(down.at[pl.ds(pl.multiple_of(xh * 896, 128), 896), :], db.at[plane(0, 0), xh], load_sem.at[2]),
    ]
    load_gate = pltpu.make_async_copy(gate.at[:, pl.ds(pl.multiple_of(xh * 896, 128), 896)], gw, load_sem.at[3])
    for load in loads:
        load.start()
    load_gate.start()
    barrier = pltpu.get_barrier_semaphore()
    for target in targets.values():
        pl.semaphore_signal(barrier, inc=1, device_id=target, device_id_type=MESH)
    pl.semaphore_wait(barrier, len(targets))
    for load in loads:
        load.wait()
    gate_waited = False
    used = []
    for what, item in order:
        if item.name[0] == "D" and what == "task":
            if len(used) >= 8:
                early = by_name["Q" + used[-8]]
                descriptor(early, early.landing).wait_send()
            slot[int(item.name[1:])] = len(used) % 8
            used.append(item.name[1:])
            by_name["Q" + used[-1]].source = psib.at[slot[int(used[-1])]]
        if what == "send":
            descriptor(item, item.landing).start()
        elif what == "recv":
            descriptor(item, item.here).wait_recv()
        else:
            if item.name[0] == "G" and not gate_waited:
                load_gate.wait()
                gate_waited = True
            item.run()
    stores = [pltpu.make_async_copy(ga, grads.at[core], load_sem.at[4]), pltpu.make_async_copy(gb, grads.at[1 - core], load_sem.at[5])]
    for store in stores:
        store.start()
    already = {"Q" + n for n in used[:-8]}
    for copy in copies:
        if copy.name not in already:
            descriptor(copy, copy.landing).wait_send()
    for store in stores:
        store.wait()


COPIES = 8 + 19 + 64 + 64 + 5 + 16 + 4 + 32 + 2


def frozen_block(tokens, gate, up, down, grad_low, grad_high, live):
    hbm = pl.BlockSpec(memory_space=pl.ANY)
    return pl.pallas_call(
        kernel,
        out_shape=(jax.ShapeDtypeStruct((128, 4096), F32), jax.ShapeDtypeStruct((2, 2, 16, 16, 1024), BF)),
        in_specs=[hbm] * 6 + [pl.BlockSpec(memory_space=pltpu.VMEM)],
        out_specs=(pl.BlockSpec(memory_space=pltpu.VMEM), hbm),
        scratch_shapes=[
            pltpu.VMEM((4, 2, 128, 4096), BF),
            pltpu.VMEM((4096, 896), BF),
            pltpu.VMEM((16, 2, 128, 896), BF),
            pltpu.VMEM((16, 2, 896, 128), BF),
            pltpu.VMEM((4, 256, 896), F32),
            pltpu.VMEM((4, 256, 896), F32),
            pltpu.VMEM((4, 256, 896), BF),
            pltpu.VMEM((8, 4, 128, 256), BF),
            pltpu.VMEM((16, 4, 128, 256), BF),
            pltpu.VMEM((16, 4, 128, 256), BF),
            pltpu.VMEM((8, 128, 256), BF),
            pltpu.VMEM((8, 128, 256), BF),
            pltpu.VMEM((16, 128, 256), BF),
            pltpu.VMEM((16, 128, 256), BF),
            pltpu.VMEM((2, 64, 896), BF),
            pltpu.VMEM((2, 448, 128), BF),
            pltpu.VMEM((2, 256, 1152), F32),
            pltpu.VMEM((2, 64, 1024), F32),
            pltpu.VMEM((8, 128), F32),
            pltpu.VMEM((2, 2, 40, 1152), F32),
            pltpu.VMEM((2, 2, 80, 1152), F32),
            pltpu.VMEM((4, 2, 16, 1152), F32),
            pltpu.VMEM((2, 16, 16, 1024), BF),
            pltpu.VMEM((2, 16, 16, 1024), BF),
            pltpu.SemaphoreType.DMA((6,)),
            pltpu.SemaphoreType.DMA((COPIES,)),
            pltpu.SemaphoreType.DMA((COPIES,)),
        ],
        compiler_params=pltpu.CompilerParams(
            collective_id=0, has_side_effects=True, vmem_limit_bytes=67_000_000),
        cost_estimate=pl.CostEstimate(flops=22_500_000_000, bytes_accessed=16_000_000, transcendentals=1_000_000),
        name="frozen_block",
    )(tokens, gate, up, down, grad_low, grad_high, live)


def shards(
    tokens,
    gate_projection_weight,
    up_projection_weight,
    down_projection_weight,
    router_projection_weight,
    adapter_down_factors,
    adapter_up_factors,
    routes,
    padding_token_mask,
    cotangent,
):
    expert_list = router_projection_weight.shape[1]
    rank_index = adapter_down_factors.shape[1] // expert_list
    logits = jnp.dot(tokens, router_projection_weight, preferred_element_type=F32)
    experts_iota = jnp.arange(expert_list, dtype=jnp.int32)[None, :]
    first_hot = (routes[:, 0:1] == experts_iota).astype(F32)
    second_hot = (routes[:, 1:2] == experts_iota).astype(F32)
    first_logit = jnp.sum(logits * first_hot, axis=1, keepdims=True)
    second_logit = jnp.sum(logits * second_hot, axis=1, keepdims=True)
    weight_first = jax.nn.sigmoid(first_logit - second_logit)
    coeff = weight_first * first_hot + (1.0 - weight_first) * second_hot
    coeff_wide = jnp.repeat(coeff, rank_index, axis=1)
    low_rank_state = jnp.dot(tokens, adapter_down_factors, preferred_element_type=F32)
    scaled_output = (low_rank_state * coeff_wide).astype(BF)
    masked_tokens = cotangent * padding_token_mask[:, None].astype(BF)
    low_rank_gradient = lax.dot_general(
        masked_tokens, adapter_up_factors, (((1,), (1,)), ((), ())), preferred_element_type=F32)
    dlow = (low_rank_gradient * coeff_wide).astype(BF)
    local_live = jnp.sum(padding_token_mask.astype(F32))
    local_up = lax.dot_general(
        scaled_output, masked_tokens, (((0,), (0,)), ((), ())), preferred_element_type=F32)
    local_down = lax.dot_general(
        dlow, tokens, (((0,), (0,)), ((), ())), preferred_element_type=F32)
    base, grads = frozen_block(
        tokens, gate_projection_weight, up_projection_weight, down_projection_weight,
        local_down, local_up, jnp.full((8, 128), local_live, F32))
    adapter_delta = jnp.dot(scaled_output, adapter_up_factors, preferred_element_type=F32)
    layer_out = (base + adapter_delta).astype(BF)
    rows = grads.reshape(2, 2, 256, 1024)
    grad_down = rows[:, :, :128].transpose(0, 1, 3, 2).reshape(4096, 128).astype(F32)
    grad_up = rows[:, :, 128:].transpose(2, 0, 1, 3).reshape(128, 4096).astype(F32)
    return (layer_out, grad_down, grad_up)


def solution(mesh):
    return jax.shard_map(
        shards,
        mesh=mesh,
        in_specs=(
            P(("dp", "blk"), None),
            P(None, "blk"),
            P("dp", "blk"),
            P("blk", "dp"),
            P(),
            P(),
            P(),
            P(("dp", "blk"), None),
            P(("dp", "blk")),
            P(("dp", "blk"), None),
        ),
        out_specs=(P(("dp", "blk"), None), P(), P()),
        check_vma=False,
    )
```

time: 201 us -> 157 us (0.78)
  Pallas kernels: 160 us -> 130 us
  between operations: 14.8 us -> 0.74 us
  other arithmetic: 8.59 us -> 2.55 us
  local copies, waits for them, and re-layouts: 4.96 us -> 10.9 us
    pallas_call x1, Pallas kernels: 160 us -> 130 us  [frozen_block(): pl.pallas_call(kernel, out_shape=(jax.ShapeDtypeStruct((128, 4096), F32),...]
    convert_element_type x0 -> x3, local copies, waits for them, and re-layouts: none -> 8.75 us  [the longest x2 6.95 us: shards(): rows[:, :, 128:].transpose(2, 0, 1, 3).reshape(128, 4096).astype(F32)]
    mul x1 -> x0, other arithmetic: 3.9 us -> none  [shards(): grad_up = packed[128:256] * inverse]
    concatenate x1 -> x0, other arithmetic: 2.6 us -> none  [shards(): jnp.concatenate([local_down, local_up, jnp.full((8, 4096), local_live, F3...]
    unnamed x9 -> x8, local copies, waits for them, and re-layouts: 2.12 us -> 0.02 us
  transfers between devices with their start and end apart: 1 -> 0, of which waited for: 1 -> 0; matrix products, arithmetic and copies ran while one was open for 2% -> 0% of each run, Pallas kernels for 80% -> 0%
where the time goes in v2:
time: 157 us; the launch traced here: 156 us
  Pallas kernels  130 us (83%)
  matrix products  11.6 us (7%)
  local copies, waits for them, and re-layouts  10.9 us (7%)
  other arithmetic  2.55 us (2%)
    pallas_call x1, Pallas kernels, frozen_block(): pl.pallas_call(kernel, out_shape=(jax.ShapeDtypeStruct((128, 4096), F32),...  130 us
    convert_element_type x2, local copies, waits for them, and re-layouts, shards(): rows[:, :, 128:].transpose(2, 0, 1, 3).reshape(128, 4096).astype(F32)  6.95 us
    dot_general x1, matrix products, shards(): jnp.dot(scaled_output, adapter_up_factors, preferred_element_type=F32)  3.45 us

profile of v2, /device:TPU:0, one launch (start us, length us, event | category | flops | bytes accessed | tf_op | source)
XLA Modules:
  0.0 155.8 jit_solution(16901007146993529281)
XLA Ops:
  0.6 0.0 copy-start
  0.6 0.0 copy-start.1
  0.7 0.0 copy-start.2
  0.7 1.4 convert_reduce_fusion
  2.1 0.7 convert_element_type.36
  2.7 0.8 slice_bitcast_fusion.1
  3.5 1.6 %select_reduce_fusion = (f32[128]{0:T(128)S(1)}, f32[128]{0:T(128)S(1)}) fusion(s32[128]{0:T(128)S(1)} %get-tuple-element.14, s32[128]{0:T(128)S(1)} %get-tuple-element.13, bf16[128,4096]{1,0:T(8,128)(2,1)} %tokens.1, bf16[4096,8]{0,1:T(8,128)(2,1)} %param.14), kind=kOutput, calls=%fused_computation.15 | convolution fusion | flops 8394496 | bytes 1116160 | tf_op jit(solution)/shard_map/dot_general | solution.py:499
  5.1 1.2 broadcast_in_dim.5.live
  6.4 0.1 copy.16
  6.5 2.0 %fusion.2 = bf16[128,128]{1,0:T(8,128)(2,1)S(1)} fusion(f32[128,128]{1,0:T(8,128)S(1)} %copy.16, bf16[128,4096]{1,0:T(8,128)(2,1)} %tokens.1, bf16[4096,128]{1,0:T(8,128)(2,1)} %param.15), kind=kOutput, calls=%fused_computation.7 | convolution fusion | flops 134250496 | bytes 2195456 | tf_op jit(solution)/shard_map/dot_general | solution.py:508
  8.5 0.0 copy-done
  8.5 0.0 copy-done.1
  8.5 0.0 copy-done.2
  8.5 2.7 %fusion.3.grad_low = f32[128,4096]{1,0:T(8,128)} fusion(bf16[128,4096]{1,0:T(8,128)(2,1)S(1)} %copy-done, f32[128,128]{0,1:T(8,128)S(1)} %bitcast.23, bf16[128,4096]{1,0:T(8,128)(2,1)S(1)} %copy-done.2, bf16[128,4096]{1,0:T(8,128)(2,1)S(1)} %copy-done.1, bf16[128]{0:T(256)(128)(2,1)S(1)} %convert_element_type.36), kind=kOutput, calls=%fused_computation.8 | convolution fusion | flops 268992512 | bytes 5308672 | tf_op jit(solution)/shard_map/dot_general | solution.py:517
  11.2 1.8 %fusion.4.grad_high = f32[128,4096]{1,0:T(8,128)} fusion(bf16[128,128]{1,0:T(8,128)(2,1)S(1)} %fusion.2, bf16[128,4096]{1,0:T(8,128)(2,1)S(1)} %copy-done.1, bf16[128]{0:T(256)(128)(2,1)S(1)} %convert_element_type.36), kind=kOutput, calls=%fused_computation.9 | convolution fusion | flops 134742016 | bytes 3178752 | tf_op jit(solution)/shard_map/dot_general | solution.py:515
  13.0 130.1 %frozen_block.1 = (f32[128,4096]{1,0:T(8,128)}, bf16[2,2,16,16,1024]{4,3,2,1,0:T(8,128)(2,1)}) custom-call(bf16[128,4096]{1,0:T(8,128)(2,1)} %tokens.1, bf16[4096,1792]{1,0:T(8,128)(2,1)} %gate.1, bf16[128,1792]{1,0:T(8,128)(2,1)} %up.1, bf16[1792,128]{1,0:T(8,128)(2,1)} %down.1, f32[128,4096]{1,0:T(8,128)} %fusion.3.grad_low, f32[128,4096]{1,0:T(8,128)} %fusion.4.grad_high, ...), custom_call_target="tpu_custom_call" | custom-call | flops 22499999744 | bytes 16000000 | tf_op jit(solution)/shard_map/frozen_block/pallas_call | solution.py:444
  143.1 0.0 copy-start.3
  143.1 3.5 %fusion = bf16[128,4096]{1,0:T(8,128)(2,1)} fusion(f32[128,4096]{1,0:T(8,128)} %get-tuple-element.5, bf16[128,128]{1,0:T(8,128)(2,1)S(1)} %fusion.2, bf16[128,4096]{1,0:T(8,128)(2,1)} %param.16), kind=kOutput, calls=%fused_computation.1 | convolution fusion | flops 135266304 | bytes 4227072 | tf_op jit(solution)/shard_map/dot_general | solution.py:522
  146.6 0.0 copy-done.3
  146.6 0.5 convert_bitcast_fusion
  147.1 2.9 %copy.18 = f32[128,2,2,1024]{3,2,1,0:T(2,128)} copy(f32[128,2,2,1024]{3,0,2,1:T(8,128)S(1)} %get-tuple-element.11) | data formatting | bytes 4194304 | tf_op jit(solution)/shard_map/convert_element_type | solution.py:526
  150.0 4.0 %reshape.43 = f32[128,4096]{1,0:T(8,128)} reshape(f32[128,2,2,1024]{3,2,1,0:T(2,128)} %copy.18) | data formatting | bytes 4194304 | tf_op jit(solution)/shard_map/convert_element_type | solution.py:526
  154.0 1.8 %copy.17 = f32[2,2,1024,128]{3,2,1,0:T(8,128)} copy(f32[2,2,1024,128]{2,3,1,0:T(8,128)S(1)} %get-tuple-element.12) | data formatting | bytes 4194304 | tf_op jit(solution)/shard_map/convert_element_type | solution.py:525
  (3 shorter events, 0.0 us)
Async XLA Ops:
  0.6 7.8 %copy-start = (bf16[128,4096]{1,0:T(8,128)(2,1)S(1)}, bf16[128,4096]{1,0:T(8,128)(2,1)}, u32[]{:S(2)}) copy-start(bf16[128,4096]{1,0:T(8,128)(2,1)} %tokens.1) | copy-start | bytes 3145732
  0.6 7.8 %copy-start.1 = (bf16[128,4096]{1,0:T(8,128)(2,1)S(1)}, bf16[128,4096]{1,0:T(8,128)(2,1)}, u32[]{:S(2)}) copy-start(bf16[128,4096]{1,0:T(8,128)(2,1)} %param.19) | copy-start | bytes 3145732
  0.7 7.8 %copy-start.2 = (bf16[128,4096]{1,0:T(8,128)(2,1)S(1)}, bf16[128,4096]{1,0:T(8,128)(2,1)}, u32[]{:S(2)}) copy-start(bf16[128,4096]{1,0:T(8,128)(2,1)} %param.16) | copy-start | bytes 3145732
  143.1 3.5 %copy-start.3 = (bf16[2,2,16,16,1024]{4,3,2,1,0:T(8,128)(2,1)S(1)}, bf16[2,2,16,16,1024]{4,3,2,1,0:T(8,128)(2,1)}, u32[]{:S(2)}) copy-start(bf16[2,2,16,16,1024]{4,3,2,1,0:T(8,128)(2,1)} %get-tuple-element.6) | copy-start | bytes 6291460

commit v3 on v2

--- a/solution.py
+++ b/solution.py
@@ -13,6 +13,7 @@
 HOP, PAIR_HOP = 1.8, 1.0
 AHEAD = 1.5
 GRAD_RANK = 50
+SLOTS = 3
 
 
 class Copy:
@@ -73,8 +74,8 @@
     return order, now
 
 
-def kernel(tokens, gate, up, down, grad_low, grad_high, live, base, grads, tok, gw, ub, db, gact, uact, hid, psib, rsib, summed,
-           rl, rr, fl, fr, ustage, dstage, g, own, live_pair, rz, rm, xs, ga, gb, load_sem, send_sem, recv_sem):
+def kernel(tokens, gate, up, down, cotangent, factors_down, factors_up, router, small, base, grads, tok, gw, ub, db, gact, uact, hid, psib, rsib, summed,
+           rl, rr, fl, fr, ustage, dstage, g, stage, cot, fdown, fup, coef, scaled, turned, rz, rm, xs, ga, gb, load_sem, send_sem, recv_sem):
     dp, blk = lax.axis_index("dp"), lax.axis_index("blk")
     z, y, xh = dp // 8, (dp // 2) % 4, dp % 2
     xl, core = blk // 2, blk % 2
@@ -161,20 +162,24 @@
 
     mib = 128 * 4096 * 2
     have_au = across("u", up, ub, ustage, 64, 0)
-    quarters = [pl.ds(32 * q, 32) for q in range(4)]
-    for sign, r, order4 in (("+", 3, (0, 1, 2, 3)), ("-", 1, (2, 3, 0, 1))):
-        for n, q in enumerate(order4):
-            part = quarters[q]
-            add("K%s%d" % (sign, q), "x" + sign, mib // 4, tok.at[0, 0, part], tok.at[r, 0, part], tok.at[r, 0, part], ["L", "Au" + sign], 3)
-            if n < 2:
-                add("KF%d" % q, "x" + sign, mib // 4, tok.at[r, 0, part], tok.at[2, 0, part], tok.at[2, 0, part], ["K%s%d" % (sign, q)], 4)
-                add("KP%d" % q, "pair", mib // 4, tok.at[2, 0, part], tok.at[2, 1, part], tok.at[2, 1, part], ["KF%d" % q])
-    came_near = {0: ["L"], 3: ["K+%d" % q for q in range(4)], 1: ["K-%d" % q for q in range(4)]}
-    for r in (0, 1, 3):
-        add("KS%d" % r, "pair", mib, tok.at[r, 0], tok.at[r, 1], tok.at[r, 1], came_near[r])
-    came_near[2] = ["KF%d" % q for q in range(4)]
-    came_pair = {r: ["KS%d" % r] for r in (0, 1, 3)}
-    came_pair[2] = ["KP%d" % q for q in range(4)]
+    def columns_of(dz):
+        return pl.ds(pl.multiple_of(((z + dz) % 4) * 1024, 1024), 1024)
+
+    def some(r, c, dz):
+        return tok.at[r, c, :, columns_of(dz)]
+
+    came_tok = {}
+    for dz in REL:
+        came_tok[0, dz] = ["L"]
+        for sign, r in (("+", 3), ("-", 1)):
+            add("K%s%d" % (sign, dz), "x" + sign, mib // 4, some(0, 0, dz), some(r, 0, dz), some(r, 0, dz), ["L", "Au" + sign], 3)
+            came_tok[r, dz] = ["K%s%d" % (sign, dz)]
+        sign, r = ("+", 3) if dz < 2 else ("-", 1)
+        add("KF%d" % dz, "x" + sign, mib // 4, some(r, 0, dz), some(2, 0, dz), some(2, 0, dz), came_tok[r, dz], 4)
+        came_tok[2, dz] = ["KF%d" % dz]
+        for r in REL:
+            add("KS%d%d" % (r, dz), "pair", mib // 4, some(r, 0, dz), some(r, 1, dz), some(r, 1, dz), came_tok[r, dz])
+            came_tok[r, dz] = came_tok[r, dz] + ["KS%d%d" % (r, dz)]
     have_ad = across("d", down, db, dstage, 448, 5)
     def piece_of(kind, own):
         return lambda dz, dy, half: weight(kind, dz, dy, own, half)
@@ -183,27 +188,28 @@
     have_up = spread("up", piece_of("u", False), piece, "z", have_au, 0)
     have_do = spread("do", piece_of("d", True), piece, "z", ["L"], 100)
     have_dp = spread("dp", piece_of("d", False), piece, "y", have_ad, 100)
-    came_tok = {r: came_near[r] + came_pair[r] for r in REL}
 
     tasks = []
 
-    def run_gate(places):
+    def run_gate(places, n, dz):
         def run():
             def step(i, carry):
-                k = pl.multiple_of(i * 512, 512)
+                k = pl.multiple_of(((z + dz) % 4) * 1024 + i * 512, 512)
                 left = jnp.concatenate([tok[r, :, :, pl.ds(k, 512)].reshape(256, 512) for r in places], axis=0)
                 part = jnp.dot(left, gw[pl.ds(k, 512), :], preferred_element_type=F32)
-                for n, r in enumerate(places):
-                    uact[r] += part[n * 256:n * 256 + 256]
+                for m, r in enumerate(places):
+                    gact[r] += part[m * 256:m * 256 + 256]
                 return carry
 
-            for r in places:
-                uact[r] = jnp.zeros((256, 896), F32)
-            lax.fori_loop(0, 8, step, 0)
-            for r in places:
-                v = uact[r]
-                gact[r] = v / (1.0 + jnp.exp(-v))
-                uact[r] = jnp.zeros((256, 896), F32)
+            if n == 0:
+                for r in places:
+                    gact[r] = jnp.zeros((256, 896), F32)
+                    uact[r] = jnp.zeros((256, 896), F32)
+            lax.fori_loop(0, 2, step, 0)
+            if n == 3:
+                for r in places:
+                    v = gact[r]
+                    gact[r] = v / (1.0 + jnp.exp(-v))
         return run
 
     def run_up(dz, dy, i):
@@ -220,13 +226,17 @@
         hid[...] = (gact[...] * uact[...]).astype(BF)
 
     ups = []
-    for name, cost, places in (("G0", 5.7, (0,)), ("G1", 9.0, (1, 3)), ("G2", 5.7, (2,))):
-        tasks.append(Task(name, cost, run_gate(places), [n for r in places for n in came_tok[r]] + ["LG"], 10))
-    for dz in range(4):
-        for dy in range(4):
+    for name, cost, places in (("G0", 1.4, (0,)), ("G1", 2.2, (1, 3)), ("G2", 1.4, (2,))):
+        for n, dz in enumerate(REL):
+            ready = [name + str(n - 1)] if n else ["LG"]
+            tasks.append(Task(name + str(n), cost, run_gate(places, n, dz), ready + [m for r in places for m in came_tok[r, dz]], 10))
+    ups = ["G03", "G13", "G23"]
+    for dz in REL:
+        for dy in REL:
             for i in (0, 1):
+                ready = have_uo(dz, dy) + have_up(dz, dy) + ["G10", "G20" if i else "G00"]
+                ready = ready + [m for r in (2 * i, 2 * i + 1) for m in came_tok[r, dz]]
                 ups.append("U%d%d%d" % (dz, dy, i))
-                ready = have_uo(dz, dy) + have_up(dz, dy) + ["G1", "G2" if i else "G0"]
                 tasks.append(Task(ups[-1], 0.45, run_up(dz, dy, i), ready, 20 + i))
     tasks.append(Task("H", 0.5, run_hidden, ups, 0))
     blocks = sorted(((dz, dy) for dz in range(4) for dy in range(4)), key=lambda p: (min(p[0], 4 - p[0]) + min(p[1], 4 - p[1]), p))
@@ -265,7 +275,9 @@
     def run_final(b, dz, dy):
         def run():
             total = summed[b, 0].astype(F32) + fl[b].astype(F32) + fr[b].astype(F32)
-            base[:, pl.ds(pl.multiple_of(plane(dz, dy) * 256, 256), 256)] = total
+            columns = pl.ds(pl.multiple_of(plane(dz, dy) * 256, 256), 256)
+            delta = jnp.dot(scaled[...], fup[:, columns], preferred_element_type=F32)
+            base[:, columns] = (total + delta).astype(BF)
         return run
 
     hidden = ["H"]
@@ -283,38 +295,62 @@
             add("N" + n, "x+", size, summed.at[b, 1], fl.at[b], fl.at[b], ["A" + n], 12 + 3 * b)
             add("M" + n, "x-", size, summed.at[b, 3], fr.at[b], fr.at[b], ["C" + n], 11 + 3 * b)
         tasks.append(Task("C" + n, 0.05, run_merge(b), ["A" + n, "Z" + n], 100 + b))
-        tasks.append(Task("E" + n, 0.1, run_final(b, dz, dy), ["A" + n, "M" + n, "N" + n], 400 + b))
+        tasks.append(Task("E" + n, 0.2, run_final(b, dz, dy), ["A" + n, "M" + n, "N" + n, "W0"], 400 + b))
 
     wide = 1152 * 4
-    pair_after = ["PL"]
-    add("PL", "pair", 4096, live, live_pair, live_pair, [], 0)
-    for ab in range(2):
-        there = pl.ds(pl.multiple_of((1 - core) * 2048 + ab * 1024, 1024), 1024)
-        for h, part in enumerate((grad_low, grad_high)):
-            landing = g.at[ab, pl.ds(h * 128, 128), pl.ds(0, 1024)]
-            add("PG%d%d" % (ab, h), "pair", 128 * 4096, part.at[:, there], landing, landing, [], 1)
-            pair_after.append("PG%d%d" % (ab, h))
-
-    def run_own():
-        parts = [(ab, h, n) for ab in range(2) for h in range(2) for n in range(2)]
-
-        def fetch(i):
-            ab, h, n = parts[i]
-            here = pl.ds(pl.multiple_of(core * 2048 + ab * 1024, 1024), 1024)
-            part = (grad_low, grad_high)[h]
-            return pltpu.make_async_copy(part.at[pl.ds(n * 64, 64), here], own.at[i % 2], load_sem.at[4 + i % 2])
-
-        fetch(0).start()
-        for i, (ab, h, n) in enumerate(parts):
-            if i + 1 < len(parts):
-                fetch(i + 1).start()
-            fetch(i).wait()
-            g[ab, h * 128 + n * 64:h * 128 + n * 64 + 64, 0:1024] += own[i % 2]
-        count = live[0:1, :] + live_pair[0:1, :]
-        for ab in range(2):
-            g[ab, :, 1024:1152] = jnp.broadcast_to(count, (256, 128))
-
-    tasks.append(Task("PA", 6.0, run_own, pair_after, 5))
+
+    def run_low():
+        mine = tok[0, 0]
+        across = (((1,), (1,)), ((), ()))
+        logits = lax.dot_general(mine, router[...], across, preferred_element_type=F32)
+        first, second = small[:, 0:1], small[:, 1:2]
+        expert = lax.broadcasted_iota(jnp.int32, (128, 8), 1)
+        first_logit = jnp.sum(jnp.where(expert == first, logits, 0.0), axis=1, keepdims=True)
+        second_logit = jnp.sum(jnp.where(expert == second, logits, 0.0), axis=1, keepdims=True)
+        weight = jax.nn.sigmoid(first_logit - second_logit)
+        column = lax.broadcasted_iota(jnp.int32, (128, 128), 1) // 16
+        wide_coef = jnp.where(column == first, weight, jnp.where(column == second, 1.0 - weight, 0.0))
+        coef[...] = wide_coef
+        low = jnp.dot(mine, fdown[...], preferred_element_type=F32)
+        value = (low * wide_coef).astype(BF)
+        scaled[...] = value
+        turned[1] = value.astype(F32).T.astype(BF)
+
+    def run_dlow():
+        cot[...] = cot[...] * small[:, 2:3].astype(F32).astype(BF)
+        low = lax.dot_general(cot[...], fup[...], (((1,), (1,)), ((), ())), preferred_element_type=F32)
+        turned[0] = (low * coef[...]).astype(BF).astype(F32).T.astype(BF)
+
+    def local_part(owner, ab, h):
+        columns = pl.ds(pl.multiple_of(owner * 2048 + ab * 1024, 1024), 1024)
+        right = cot[:, columns] if h else tok[0, 0, :, columns]
+        return jnp.dot(turned[h], right, preferred_element_type=F32)
+
+    def count():
+        return jnp.broadcast_to(jnp.sum(small[:, 2:3].astype(F32), axis=0, keepdims=True), (128, 128))
+
+    tasks.append(Task("W0", 3.5, run_low, ["L", "LC"], 3))
+    tasks.append(Task("W1", 2.5, run_dlow, ["W0"], 3))
+    pieces = [(ab, h) for ab in range(2) for h in range(2)]
+    for n, (ab, h) in enumerate(pieces):
+        name = "PG%d%d" % (ab, h)
+
+        def run_theirs(n=n, ab=ab, h=h):
+            if n >= 2:
+                early = by_name["PG%d%d" % pieces[n - 2]]
+                descriptor(early, early.landing).wait_send()
+            stage[n % 2, :, 0:1024] = local_part(1 - core, ab, h)
+            stage[n % 2, :, 1024:1152] = count()
+
+        def run_ours(ab=ab, h=h):
+            rows = slice(h * 128, h * 128 + 128)
+            g[ab, rows, 0:1024] += local_part(core, ab, h)
+            g[ab, rows, 1024:1152] += count()
+
+        landing = g.at[ab, pl.ds(h * 128, 128)]
+        tasks.append(Task("WS%d%d" % (ab, h), 0.5, run_theirs, ["W1"] + (["WS%d%d" % pieces[n - 1]] if n else []), 3))
+        add(name, "pair", 128 * wide, stage.at[n % 2], landing, landing, ["WS%d%d" % (ab, h)], 1)
+        tasks.append(Task("WO%d%d" % (ab, h), 0.5, run_ours, [name, "W1"], 4))
 
     def reduce_ring(tag, axis, piece_at, hold_z, hold_m, rows, after, finish, rank):
         amount = rows * wide
@@ -337,7 +373,7 @@
             rows = pl.multiple_of(((p + d) % 4) * 64 + (half or 0) * 32, 32)
             return g.at[ab, pl.ds(rows, 64 if half is None else 32)]
 
-        def small(d, half=None, ab=ab, p=p, q=q):
+        def slim(d, half=None, ab=ab, p=p, q=q):
             rows = pl.multiple_of(p * 64 + ((q + d) % 4) * 16 + (half or 0) * 8, 8)
             return g.at[ab, pl.ds(rows, 16 if half is None else 8)]
 
@@ -348,11 +384,11 @@
             ref = block(0)
             ref[...] = ref[...] + rm[ab, 0, 0:64] + rm[ab, 1, 0:64]
 
-        def second_done(small=small, ab=ab):
-            xs[0, ab] = small(0)[...] + rm[ab, 0, 64:80] + rm[ab, 1, 64:80]
-
-        reduce_ring("R%d" % ab, first, block, z1, m1, 64, ["PA"], first_done, GRAD_RANK)
-        reduce_ring("S%d" % ab, second, small, z2, m2, 16, ["R%dE" % ab], second_done, GRAD_RANK)
+        def second_done(slim=slim, ab=ab):
+            xs[0, ab] = slim(0)[...] + rm[ab, 0, 64:80] + rm[ab, 1, 64:80]
+
+        reduce_ring("R%d" % ab, first, block, z1, m1, 64, ["WO%d0" % ab, "WO%d1" % ab], first_done, GRAD_RANK)
+        reduce_ring("S%d" % ab, second, slim, z2, m2, 16, ["R%dE" % ab], second_done, GRAD_RANK)
 
     slices = ["S0E", "S1E"]
     add("X+", "x+", 32 * wide, xs.at[0], xs.at[3], xs.at[3], slices, 6)
@@ -380,7 +416,7 @@
         whole = sorted({n for dz in range(4) for dy in range(4) for n in have(dz, dy)})
         add("PH%d" % ab, "pair", 256 * 1024 * 2, ga.at[ab], gb.at[ab], gb.at[ab], whole)
 
-    order, _ = arrange(copies, tasks, ["L", "LG"])
+    order, _ = arrange(copies, tasks, ["L", "LG", "LC"])
     assert len(copies) == COPIES
     place = {copy.name: i for i, copy in enumerate(copies)}
     by_name = {copy.name: copy for copy in copies}
@@ -397,7 +433,14 @@
         pltpu.make_async_copy(down.at[pl.ds(pl.multiple_of(xh * 896, 128), 896), :], db.at[plane(0, 0), xh], load_sem.at[2]),
     ]
     load_gate = pltpu.make_async_copy(gate.at[:, pl.ds(pl.multiple_of(xh * 896, 128), 896)], gw, load_sem.at[3])
+    extra = [
+        pltpu.make_async_copy(cotangent, cot, load_sem.at[4]),
+        pltpu.make_async_copy(factors_down, fdown, load_sem.at[5]),
+        pltpu.make_async_copy(factors_up, fup, load_sem.at[6]),
+    ]
     for load in loads:
+        load.start()
+    for load in extra:
         load.start()
     load_gate.start()
     barrier = pltpu.get_barrier_semaphore()
@@ -410,10 +453,10 @@
     used = []
     for what, item in order:
         if item.name[0] == "D" and what == "task":
-            if len(used) >= 8:
-                early = by_name["Q" + used[-8]]
+            if len(used) >= SLOTS:
+                early = by_name["Q" + used[-SLOTS]]
                 descriptor(early, early.landing).wait_send()
-            slot[int(item.name[1:])] = len(used) % 8
+            slot[int(item.name[1:])] = len(used) % SLOTS
             used.append(item.name[1:])
             by_name["Q" + used[-1]].source = psib.at[slot[int(used[-1])]]
         if what == "send":
@@ -424,11 +467,18 @@
             if item.name[0] == "G" and not gate_waited:
                 load_gate.wait()
                 gate_waited = True
+            if item.name == "W0":
+                for load in extra:
+                    load.wait()
             item.run()
-    stores = [pltpu.make_async_copy(ga, grads.at[core], load_sem.at[4]), pltpu.make_async_copy(gb, grads.at[1 - core], load_sem.at[5])]
+    stores = []
+    for n, (half, whole) in enumerate(((core, ga), (1 - core, gb))):
+        for ab in range(2):
+            columns = pl.ds(pl.multiple_of(half * 2048 + ab * 1024, 1024), 1024)
+            stores.append(pltpu.make_async_copy(whole.at[ab], grads.at[:, :, columns], load_sem.at[2 * n + ab]))
     for store in stores:
         store.start()
-    already = {"Q" + n for n in used[:-8]}
+    already = {"Q" + n for n in used[:-SLOTS]} | {"PG00", "PG01"}
     for copy in copies:
         if copy.name not in already:
             descriptor(copy, copy.landing).wait_send()
@@ -436,15 +486,15 @@
         store.wait()
 
 
-COPIES = 8 + 19 + 64 + 64 + 5 + 16 + 4 + 32 + 2
-
-
-def frozen_block(tokens, gate, up, down, grad_low, grad_high, live):
+COPIES = 8 + 28 + 64 + 64 + 4 + 16 + 4 + 32 + 2
+
+
+def layer(*operands):
     hbm = pl.BlockSpec(memory_space=pl.ANY)
     return pl.pallas_call(
         kernel,
-        out_shape=(jax.ShapeDtypeStruct((128, 4096), F32), jax.ShapeDtypeStruct((2, 2, 16, 16, 1024), BF)),
-        in_specs=[hbm] * 6 + [pl.BlockSpec(memory_space=pltpu.VMEM)],
+        out_shape=(jax.ShapeDtypeStruct((128, 4096), BF), jax.ShapeDtypeStruct((16, 16, 4096), BF)),
+        in_specs=[hbm] * 7 + [pl.BlockSpec(memory_space=pltpu.VMEM)] * 2,
         out_specs=(pl.BlockSpec(memory_space=pltpu.VMEM), hbm),
         scratch_shapes=[
             pltpu.VMEM((4, 2, 128, 4096), BF),
@@ -454,7 +504,7 @@
             pltpu.VMEM((4, 256, 896), F32),
             pltpu.VMEM((4, 256, 896), F32),
             pltpu.VMEM((4, 256, 896), BF),
-            pltpu.VMEM((8, 4, 128, 256), BF),
+            pltpu.VMEM((SLOTS, 4, 128, 256), BF),
             pltpu.VMEM((16, 4, 128, 256), BF),
             pltpu.VMEM((16, 4, 128, 256), BF),
             pltpu.VMEM((8, 128, 256), BF),
@@ -464,22 +514,27 @@
             pltpu.VMEM((2, 64, 896), BF),
             pltpu.VMEM((2, 448, 128), BF),
             pltpu.VMEM((2, 256, 1152), F32),
-            pltpu.VMEM((2, 64, 1024), F32),
-            pltpu.VMEM((8, 128), F32),
+            pltpu.VMEM((2, 128, 1152), F32),
+            pltpu.VMEM((128, 4096), BF),
+            pltpu.VMEM((4096, 128), BF),
+            pltpu.VMEM((128, 4096), BF),
+            pltpu.VMEM((128, 128), F32),
+            pltpu.VMEM((128, 128), BF),
+            pltpu.VMEM((2, 128, 128), BF),
             pltpu.VMEM((2, 2, 40, 1152), F32),
             pltpu.VMEM((2, 2, 80, 1152), F32),
             pltpu.VMEM((4, 2, 16, 1152), F32),
             pltpu.VMEM((2, 16, 16, 1024), BF),
             pltpu.VMEM((2, 16, 16, 1024), BF),
-            pltpu.SemaphoreType.DMA((6,)),
+            pltpu.SemaphoreType.DMA((7,)),
             pltpu.SemaphoreType.DMA((COPIES,)),
             pltpu.SemaphoreType.DMA((COPIES,)),
         ],
         compiler_params=pltpu.CompilerParams(
             collective_id=0, has_side_effects=True, vmem_limit_bytes=67_000_000),
         cost_estimate=pl.CostEstimate(flops=22_500_000_000, bytes_accessed=16_000_000, transcendentals=1_000_000),
-        name="frozen_block",
-    )(tokens, gate, up, down, grad_low, grad_high, live)
+        name="layer",
+    )(*operands)
 
 
 def shards(
@@ -494,36 +549,13 @@
     padding_token_mask,
     cotangent,
 ):
-    expert_list = router_projection_weight.shape[1]
-    rank_index = adapter_down_factors.shape[1] // expert_list
-    logits = jnp.dot(tokens, router_projection_weight, preferred_element_type=F32)
-    experts_iota = jnp.arange(expert_list, dtype=jnp.int32)[None, :]
-    first_hot = (routes[:, 0:1] == experts_iota).astype(F32)
-    second_hot = (routes[:, 1:2] == experts_iota).astype(F32)
-    first_logit = jnp.sum(logits * first_hot, axis=1, keepdims=True)
-    second_logit = jnp.sum(logits * second_hot, axis=1, keepdims=True)
-    weight_first = jax.nn.sigmoid(first_logit - second_logit)
-    coeff = weight_first * first_hot + (1.0 - weight_first) * second_hot
-    coeff_wide = jnp.repeat(coeff, rank_index, axis=1)
-    low_rank_state = jnp.dot(tokens, adapter_down_factors, preferred_element_type=F32)
-    scaled_output = (low_rank_state * coeff_wide).astype(BF)
-    masked_tokens = cotangent * padding_token_mask[:, None].astype(BF)
-    low_rank_gradient = lax.dot_general(
-        masked_tokens, adapter_up_factors, (((1,), (1,)), ((), ())), preferred_element_type=F32)
-    dlow = (low_rank_gradient * coeff_wide).astype(BF)
-    local_live = jnp.sum(padding_token_mask.astype(F32))
-    local_up = lax.dot_general(
-        scaled_output, masked_tokens, (((0,), (0,)), ((), ())), preferred_element_type=F32)
-    local_down = lax.dot_general(
-        dlow, tokens, (((0,), (0,)), ((), ())), preferred_element_type=F32)
-    base, grads = frozen_block(
+    small = jnp.concatenate([routes, padding_token_mask[:, None]], axis=1)
+    layer_out, grads = layer(
         tokens, gate_projection_weight, up_projection_weight, down_projection_weight,
-        local_down, local_up, jnp.full((8, 128), local_live, F32))
-    adapter_delta = jnp.dot(scaled_output, adapter_up_factors, preferred_element_type=F32)
-    layer_out = (base + adapter_delta).astype(BF)
-    rows = grads.reshape(2, 2, 256, 1024)
-    grad_down = rows[:, :, :128].transpose(0, 1, 3, 2).reshape(4096, 128).astype(F32)
-    grad_up = rows[:, :, 128:].transpose(2, 0, 1, 3).reshape(128, 4096).astype(F32)
+        cotangent, adapter_down_factors, adapter_up_factors, router_projection_weight.T, small)
+    rows = grads.reshape(256, 4096)
+    grad_down = rows[:128].astype(F32).T
+    grad_up = rows[128:].astype(F32)
     return (layer_out, grad_down, grad_up)
 
 

time: 157 us -> 131 us (0.83)
  matrix products: 11.6 us -> 0 us
  Pallas kernels: 130 us -> 123 us
  local copies, waits for them, and re-layouts: 10.9 us -> 5.2 us
    dot_general x5 -> x0, matrix products: 11.6 us -> none  [the longest x1 3.45 us: shards(): jnp.dot(scaled_output, adapter_up_factors, preferred_element_type=F32)]
    convert_element_type x3 -> x0, local copies, waits for them, and re-layouts: 8.75 us -> none  [the longest x2 6.95 us: shards(): rows[:, :, 128:].transpose(2, 0, 1, 3).reshape(128, 4096).astype(F32)]
    pallas_call x1, Pallas kernels: 130 us -> 123 us  [layer(): pl.pallas_call(kernel, out_shape=(jax.ShapeDtypeStruct((128, 4096), BF),...]
    transpose x0 -> x1, local copies, waits for them, and re-layouts: none -> 1.8 us  [shards(): grad_down = rows[:128].astype(F32).T]
    slice x0 -> x1, local copies, waits for them, and re-layouts: none -> 1.68 us  [shards(): grad_up = rows[128:].astype(F32)]
where the time goes in v3:
time: 131 us
  Pallas kernels  123 us (94%)
  local copies, waits for them, and re-layouts  5.2 us (4%)
  other arithmetic  2.63 us (2%)
    pallas_call x1, Pallas kernels, layer(): pl.pallas_call(kernel, out_shape=(jax.ShapeDtypeStruct((128, 4096), BF),...  123 us

profile of v3, /device:TPU:0, one launch (start us, length us, event | category | flops | bytes accessed | tf_op | source)
XLA Modules:
  0.0 131.2 jit_solution(8461079484410223485)
XLA Ops:
  0.6 0.7 pad_add_fusion
  1.3 0.7 copy.16.small
  2.1 122.7 %layer.1 = (bf16[128,4096]{1,0:T(8,128)(2,1)}, bf16[16,16,4096]{2,1,0:T(8,128)(2,1)}) custom-call(bf16[128,4096]{1,0:T(8,128)(2,1)} %tokens.1, bf16[4096,1792]{1,0:T(8,128)(2,1)} %gate.1, bf16[128,1792]{1,0:T(8,128)(2,1)} %up.1, bf16[1792,128]{1,0:T(8,128)(2,1)} %down.1, bf16[128,4096]{1,0:T(8,128)(2,1)} %cotangent.1, bf16[4096,128]{1,0:T(8,128)(2,1)} %factors_down.1, ...), custom_call_target="tpu_custom_call" | custom-call | flops 22499999744 | bytes 16000000 | tf_op jit(solution)/shard_map/layer/pallas_call | solution.py:494
  124.8 1.7 %fusion = (bf16[8,16,4096]{2,1,0:T(8,128)(2,1)S(1)}, bf16[8,16,4096]{2,1,0:T(8,128)(2,1)S(1)}) fusion(bf16[16,16,4096]{2,1,0:T(8,128)(2,1)} %get-tuple-element.6), kind=kLoop, calls=%fused_computation.3 | loop fusion | bytes 4194304 | tf_op jit(solution)/shard_map/slice | solution.py:558
  126.4 1.9 %bitcast_convert_fusion = (f32[128,4096]{1,0:T(8,128)}, f32[128,4096]{1,0:T(8,128)S(1)}) fusion(bf16[8,16,4096]{2,1,0:T(8,128)(2,1)S(1)} %get-tuple-element.7, bf16[8,16,4096]{2,1,0:T(8,128)(2,1)S(1)} %get-tuple-element.8), kind=kLoop, calls=%fused_computation | loop fusion | flops 1048576 | bytes 6291456 | tf_op jit(solution)/shard_map/convert_element_type | solution.py:558
  128.4 0.0 copy-start
  128.4 1.8 %copy.17 = f32[128,4096]{0,1:T(8,128)} copy(f32[128,4096]{1,0:T(8,128)S(1)} %get-tuple-element.10) | data formatting | bytes 4194304 | tf_op jit(solution)/shard_map/transpose | solution.py:557
  130.2 0.0 copy-done
  130.2 1.0 copy.19
Async XLA Ops:
  128.4 1.8 %copy-start = (bf16[128,4096]{1,0:T(8,128)(2,1)S(1)}, bf16[128,4096]{1,0:T(8,128)(2,1)}, u32[]{:S(2)}) copy-start(bf16[128,4096]{1,0:T(8,128)(2,1)} %get-tuple-element.14) | copy-start | bytes 3145732

commit v4 on v3

--- a/solution.py
+++ b/solution.py
@@ -11,9 +11,31 @@
 REL = (0, 1, 3, 2)
 LINK_RATE, PAIR_RATE = 46.6e3, 300e3
 HOP, PAIR_HOP = 1.8, 1.0
-AHEAD = 1.5
+AHEAD = 2.5
 GRAD_RANK = 50
 SLOTS = 3
+
+
+COPY_RANKS = (
+    -1035, -564, -297, -1186, 1297, -323, 83, -1833, 1126, 2034, 74, 1002, -117, -115, -1310, 2730, -2076, -686, 1585, 164, 950, -354, 945, 1560,
+    -262, 1893, 573, -2310, -928, 441, -1189, -117, -688, 2744, 995, 3082, 29, 1463, 411, -1001, -1815, 1111, 167, -1630, -161, -105, 1228, 805,
+    337, -717, -300, 1439, -1755, -1329, 1111, -245, -427, -477, -193, 397, 409, 915, 1009, -310, -571, -1651, -684, -542, 459, -1420, 227, -1145,
+    290, 2251, 1456, -337, 2771, 2945, 3560, 2121, 232, -953, -1179, 495, 1369, 110, -1722, -1659, 1144, 630, 2707, -270, -1954, 461, 703, -999,
+    -562, -908, 1400, 1249, 534, -173, -2003, -144, -787, 363, -21, -1398, 1473, 27, 714, 433, -741, 470, 1795, -1568, 727, -969, -721, -177,
+    -1276, -13, 2564, 3224, 39, 620, 1402, -962, -1736, 715, 785, 1952, 934, -1287, -1151, 1553, 807, -1691, 209, 2356, 466, -1055, 533, -106,
+    931, 2818, -2301, 1912, 2921, -956, 195, 1857, 2449, 1351, 683, 623, 620, 1382, -1203, 580, -344, 58, 328, 63, 1143, 498, -1147, 13,
+    810, 1313, 256, -132, -421, -674, 946, 1349, 226, 1417, 209, 320, 314, 43, 917, -362, 1870, -1583, -1719, -301, 615, -1421, -106, 655,
+    652, -898, -451, 85, -650, 855, 1004, 800, 273, -2679, 553, 1105, 1057, -175, 284, -1020, -118, 1689, 1643, -206, 1655, 322, -1652, 325,
+    -334, 1821, -332, -622, 1228, 2296,
+)
+TASK_RANKS = (
+    -33, -1131, 1174, 1480, 1485, -2499, 257, -1955, -430, 1137, 287, 345, -2437, -385, 2439, 2912, -415, -1261, 1884, -1054, 293, 2581, -656, -5095,
+    -347, 524, -2374, 2182, 455, 1020, -366, -2587, -2489, -622, -2566, -321, -3481, -4440, -106, -5293, 1667, -2396, 591, 294, -1230, 1401, -721, 171,
+    1110, 385, -1132, -2307, -715, 1876, 2225, -1705, -2537, 662, 699, 2304, 192, 905, 475, 828, -1543, 2065, 417, 2995, 1855, -1717, -2158, -210,
+    3577, 2676, -837, 944, 1596, 2779, -2082, -811, 414, 398, -425, 778, -633, 1703, 792, -1676, -656, 1519, 1951, 206, 1324, 1066, -56, -2582,
+    -239, 2270, -2355, 2041, -637, 606, 1027, 1011, 158, 2195, 194, 2230, -4962, 2123, 476, 170, 2020, 1369, -1719, -1455, 2186, 850, -1015, 506,
+    997, -1799, 754, -543, 1685, -2714, -393, -975, -237, 74, 1887, 2352,
+)
 
 
 class Copy:
@@ -74,7 +96,7 @@
     return order, now
 
 
-def kernel(tokens, gate, up, down, cotangent, factors_down, factors_up, router, small, base, grads, tok, gw, ub, db, gact, uact, hid, psib, rsib, summed,
+def kernel(tokens, gate, up, down, cotangent, factors_down, factors_up, router, small, base, grads_low, grads_high, tok, gw, ub, db, gact, uact, hid, psib, rsib, summed,
            rl, rr, fl, fr, ustage, dstage, g, stage, cot, fdown, fup, coef, scaled, turned, rz, rm, xs, ga, gb, load_sem, send_sem, recv_sem):
     dp, blk = lax.axis_index("dp"), lax.axis_index("blk")
     z, y, xh = dp // 8, (dp // 2) % 4, dp % 2
@@ -416,6 +438,10 @@
         whole = sorted({n for dz in range(4) for dy in range(4) for n in have(dz, dy)})
         add("PH%d" % ab, "pair", 256 * 1024 * 2, ga.at[ab], gb.at[ab], gb.at[ab], whole)
 
+    for item, rank in zip(copies + tasks, COPY_RANKS + TASK_RANKS, strict=True):
+        item.rank = rank
+    for item, rank in zip(copies + tasks, COPY_RANKS + TASK_RANKS, strict=True):
+        item.rank = rank
     order, _ = arrange(copies, tasks, ["L", "LG", "LC"])
     assert len(copies) == COPIES
     place = {copy.name: i for i, copy in enumerate(copies)}
@@ -472,10 +498,12 @@
                     load.wait()
             item.run()
     stores = []
-    for n, (half, whole) in enumerate(((core, ga), (1 - core, gb))):
+    for half, whole in ((core, ga), (1 - core, gb)):
         for ab in range(2):
             columns = pl.ds(pl.multiple_of(half * 2048 + ab * 1024, 1024), 1024)
-            stores.append(pltpu.make_async_copy(whole.at[ab], grads.at[:, :, columns], load_sem.at[2 * n + ab]))
+            for n, result in enumerate((grads_low, grads_high)):
+                part = whole.at[ab, pl.ds(8 * n, 8)]
+                stores.append(pltpu.make_async_copy(part, result.at[:, :, columns], load_sem.at[len(stores)]))
     for store in stores:
         store.start()
     already = {"Q" + n for n in used[:-SLOTS]} | {"PG00", "PG01"}
@@ -493,9 +521,9 @@
     hbm = pl.BlockSpec(memory_space=pl.ANY)
     return pl.pallas_call(
         kernel,
-        out_shape=(jax.ShapeDtypeStruct((128, 4096), BF), jax.ShapeDtypeStruct((16, 16, 4096), BF)),
+        out_shape=(jax.ShapeDtypeStruct((128, 4096), BF), jax.ShapeDtypeStruct((8, 16, 4096), BF), jax.ShapeDtypeStruct((8, 16, 4096), BF)),
         in_specs=[hbm] * 7 + [pl.BlockSpec(memory_space=pltpu.VMEM)] * 2,
-        out_specs=(pl.BlockSpec(memory_space=pltpu.VMEM), hbm),
+        out_specs=(pl.BlockSpec(memory_space=pltpu.VMEM), hbm, hbm),
         scratch_shapes=[
             pltpu.VMEM((4, 2, 128, 4096), BF),
             pltpu.VMEM((4096, 896), BF),
@@ -526,7 +554,7 @@
             pltpu.VMEM((4, 2, 16, 1152), F32),
             pltpu.VMEM((2, 16, 16, 1024), BF),
             pltpu.VMEM((2, 16, 16, 1024), BF),
-            pltpu.SemaphoreType.DMA((7,)),
+            pltpu.SemaphoreType.DMA((8,)),
             pltpu.SemaphoreType.DMA((COPIES,)),
             pltpu.SemaphoreType.DMA((COPIES,)),
         ],
@@ -550,12 +578,12 @@
     cotangent,
 ):
     small = jnp.concatenate([routes, padding_token_mask[:, None]], axis=1)
-    layer_out, grads = layer(
+    layer_out, grads_low, grads_high = layer(
         tokens, gate_projection_weight, up_projection_weight, down_projection_weight,
         cotangent, adapter_down_factors, adapter_up_factors, router_projection_weight.T, small)
-    rows = grads.reshape(256, 4096)
-    grad_down = rows[:128].astype(F32).T
-    grad_up = rows[128:].astype(F32)
+    unit = jnp.eye(128, dtype=BF)
+    grad_down = lax.dot_general(grads_low.reshape(128, 4096), unit, (((0,), (0,)), ((), ())), preferred_element_type=F32)
+    grad_up = grads_high.reshape(128, 4096).astype(F32)
     return (layer_out, grad_down, grad_up)
 
 

time: 131 us -> 127 us (0.969)
  Pallas kernels: 123 us -> 119 us
  local copies, waits for them, and re-layouts: 5.2 us -> 1.72 us
  matrix products: 0 us -> 3.1 us
    pallas_call x1, Pallas kernels: 123 us -> 119 us  [layer(): pl.pallas_call(kernel, out_shape=(jax.ShapeDtypeStruct((128, 4096), BF),...]
    dot_general x0 -> x1, matrix products: none -> 3.1 us  [shards(): lax.dot_general(grads_low.reshape(128, 4096), unit, (((0,), (0,)), ((), (...]
    transpose x1 -> x0, local copies, waits for them, and re-layouts: 1.8 us -> none  [shards(): grad_down = rows[:128].astype(F32).T]
    slice x1 -> x0, local copies, waits for them, and re-layouts: 1.68 us -> none  [shards(): grad_up = rows[128:].astype(F32)]
where the time goes in v4:
time: 127 us
  Pallas kernels  119 us (94%)
  matrix products  3.1 us (2%)
  other arithmetic  2.31 us (2%)
  local copies, waits for them, and re-layouts  1.72 us (1%)
    pallas_call x1, Pallas kernels, layer(): pl.pallas_call(kernel, out_shape=(jax.ShapeDtypeStruct((128, 4096), BF),...  119 us
    dot_general x1, matrix products, shards(): lax.dot_general(grads_low.reshape(128, 4096), unit, (((0,), (0,)), ((), (...  3.1 us

profile of v4, /device:TPU:0, one launch (start us, length us, event | category | flops | bytes accessed | tf_op | source)
XLA Modules:
  0.0 126.7 jit_solution(5626925235915191007)
XLA Ops:
  0.6 0.7 pad_add_fusion
  1.3 0.7 copy.15.small
  2.1 118.9 %layer.1 = (bf16[128,4096]{1,0:T(8,128)(2,1)}, bf16[8,16,4096]{2,1,0:T(8,128)(2,1)}, bf16[8,16,4096]{2,1,0:T(8,128)(2,1)}) custom-call(bf16[128,4096]{1,0:T(8,128)(2,1)} %tokens.1, bf16[4096,1792]{1,0:T(8,128)(2,1)} %gate.1, bf16[128,1792]{1,0:T(8,128)(2,1)} %up.1, bf16[1792,128]{1,0:T(8,128)(2,1)} %down.1, bf16[128,4096]{1,0:T(8,128)(2,1)} %cotangent.1, ...), custom_call_target="tpu_custom_call" | custom-call | flops 22499999744 | bytes 16000000 | tf_op jit(solution)/shard_map/layer/pallas_call | solution.py:522
  121.0 0.0 copy-start
  121.0 3.1 %fusion = f32[4096,128]{1,0:T(8,128)} fusion(bf16[128,4096]{1,0:T(8,128)(2,1)} %bitcast.7), kind=kOutput, calls=%fused_computation.2 | convolution fusion | flops 134234112 | bytes 3145728 | tf_op jit(solution)/shard_map/dot_general | solution.py:585
  124.2 0.0 copy-done
  124.2 0.0 copy-start.1
  124.2 1.6 %bitcast_convert_fusion = f32[128,4096]{1,0:T(8,128)} fusion(bf16[8,16,4096]{2,1,0:T(8,128)(2,1)S(1)} %copy-done), kind=kLoop, calls=%fused_computation | loop fusion | flops 524288 | bytes 3145728 | tf_op jit(solution)/shard_map/convert_element_type | solution.py:586
  125.8 0.0 copy-done.1
  125.8 1.0 copy.17
Async XLA Ops:
  121.0 3.1 %copy-start = (bf16[8,16,4096]{2,1,0:T(8,128)(2,1)S(1)}, bf16[8,16,4096]{2,1,0:T(8,128)(2,1)}, u32[]{:S(2)}) copy-start(bf16[8,16,4096]{2,1,0:T(8,128)(2,1)} %get-tuple-element.8) | copy-start | bytes 3145732
  124.2 1.6 %copy-start.1 = (bf16[128,4096]{1,0:T(8,128)(2,1)S(1)}, bf16[128,4096]{1,0:T(8,128)(2,1)}, u32[]{:S(2)}) copy-start(bf16[128,4096]{1,0:T(8,128)(2,1)} %get-tuple-element.12) | copy-start | bytes 3145732

commit v5 on v4

--- a/solution.py
+++ b/solution.py
@@ -96,7 +96,7 @@
     return order, now
 
 
-def kernel(tokens, gate, up, down, cotangent, factors_down, factors_up, router, small, base, grads_low, grads_high, tok, gw, ub, db, gact, uact, hid, psib, rsib, summed,
+def kernel(tokens, gate, up, down, cotangent, factors_down, factors_up, router, routes, mask, base, grads_low, grads_high, tok, gw, ub, db, gact, uact, hid, psib, rsib, summed,
            rl, rr, fl, fr, ustage, dstage, g, stage, cot, fdown, fup, coef, scaled, turned, rz, rm, xs, ga, gb, load_sem, send_sem, recv_sem):
     dp, blk = lax.axis_index("dp"), lax.axis_index("blk")
     z, y, xh = dp // 8, (dp // 2) % 4, dp % 2
@@ -269,9 +269,9 @@
     def run_down(b, dz, dy):
         def run():
             j = plane(dz, dy)
-            right = jnp.concatenate([db[j, 0], db[j, 1]], axis=1)
 
             def step(i, carry):
+                right = jnp.concatenate([db[j, 0], db[j, 1]], axis=1)
                 left = hid[pl.ds(i * 2, 2)].reshape(512, 896)
                 part = jnp.dot(left, right, preferred_element_type=F32).astype(BF).reshape(2, 2, 128, 256)
                 summed[b, pl.ds(i * 2, 2)] = part[:, 0]
@@ -321,16 +321,19 @@
 
     wide = 1152 * 4
 
+    def upright(row):
+        return jnp.broadcast_to(row.astype(F32), (128, 128)).T
+
     def run_low():
         mine = tok[0, 0]
         across = (((1,), (1,)), ((), ()))
         logits = lax.dot_general(mine, router[...], across, preferred_element_type=F32)
-        first, second = small[:, 0:1], small[:, 1:2]
-        expert = lax.broadcasted_iota(jnp.int32, (128, 8), 1)
-        first_logit = jnp.sum(jnp.where(expert == first, logits, 0.0), axis=1, keepdims=True)
-        second_logit = jnp.sum(jnp.where(expert == second, logits, 0.0), axis=1, keepdims=True)
+        first, second = upright(routes[0:1, :]), upright(routes[1:2, :])
+        expert = lax.broadcasted_iota(jnp.int32, (128, 8), 1).astype(F32)
+        first_logit = jnp.sum(jnp.where(expert == first[:, 0:8], logits, 0.0), axis=1, keepdims=True)
+        second_logit = jnp.sum(jnp.where(expert == second[:, 0:8], logits, 0.0), axis=1, keepdims=True)
         weight = jax.nn.sigmoid(first_logit - second_logit)
-        column = lax.broadcasted_iota(jnp.int32, (128, 128), 1) // 16
+        column = (lax.broadcasted_iota(jnp.int32, (128, 128), 1) // 16).astype(F32)
         wide_coef = jnp.where(column == first, weight, jnp.where(column == second, 1.0 - weight, 0.0))
         coef[...] = wide_coef
         low = jnp.dot(mine, fdown[...], preferred_element_type=F32)
@@ -339,7 +342,7 @@
         turned[1] = value.astype(F32).T.astype(BF)
 
     def run_dlow():
-        cot[...] = cot[...] * small[:, 2:3].astype(F32).astype(BF)
+        cot[...] = cot[...] * upright(mask[...])[:, 0:1].astype(BF)
         low = lax.dot_general(cot[...], fup[...], (((1,), (1,)), ((), ())), preferred_element_type=F32)
         turned[0] = (low * coef[...]).astype(BF).astype(F32).T.astype(BF)
 
@@ -349,7 +352,7 @@
         return jnp.dot(turned[h], right, preferred_element_type=F32)
 
     def count():
-        return jnp.broadcast_to(jnp.sum(small[:, 2:3].astype(F32), axis=0, keepdims=True), (128, 128))
+        return jnp.broadcast_to(jnp.sum(mask[...].astype(F32), axis=1, keepdims=True), (128, 128))
 
     tasks.append(Task("W0", 3.5, run_low, ["L", "LC"], 3))
     tasks.append(Task("W1", 2.5, run_dlow, ["W0"], 3))
@@ -522,7 +525,7 @@
     return pl.pallas_call(
         kernel,
         out_shape=(jax.ShapeDtypeStruct((128, 4096), BF), jax.ShapeDtypeStruct((8, 16, 4096), BF), jax.ShapeDtypeStruct((8, 16, 4096), BF)),
-        in_specs=[hbm] * 7 + [pl.BlockSpec(memory_space=pltpu.VMEM)] * 2,
+        in_specs=[hbm] * 7 + [pl.BlockSpec(memory_space=pltpu.VMEM)] * 3,
         out_specs=(pl.BlockSpec(memory_space=pltpu.VMEM), hbm, hbm),
         scratch_shapes=[
             pltpu.VMEM((4, 2, 128, 4096), BF),
@@ -577,10 +580,10 @@
     padding_token_mask,
     cotangent,
 ):
-    small = jnp.concatenate([routes, padding_token_mask[:, None]], axis=1)
     layer_out, grads_low, grads_high = layer(
         tokens, gate_projection_weight, up_projection_weight, down_projection_weight,
-        cotangent, adapter_down_factors, adapter_up_factors, router_projection_weight.T, small)
+        cotangent, adapter_down_factors, adapter_up_factors, router_projection_weight.T, routes.T,
+        padding_token_mask[None, :])
     unit = jnp.eye(128, dtype=BF)
     grad_down = lax.dot_general(grads_low.reshape(128, 4096), unit, (((0,), (0,)), ((), ())), preferred_element_type=F32)
     grad_up = grads_high.reshape(128, 4096).astype(F32)

time: 127 us -> 125 us (0.984)
  no operation moved by 1% of the time
where the time goes in v5:
time: 125 us
  Pallas kernels  119 us (95%)
  matrix products  3.1 us (2%)
  other arithmetic  1.6 us (1%)
    pallas_call x1, Pallas kernels, layer(): pl.pallas_call(kernel, out_shape=(jax.ShapeDtypeStruct((128, 4096), BF),...  119 us
    dot_general x1, matrix products, shards(): lax.dot_general(grads_low.reshape(128, 4096), unit, (((0,), (0,)), ((), (...  3.1 us

profile of v5, /device:TPU:0, one launch (start us, length us, event | category | flops | bytes accessed | tf_op | source)
XLA Modules:
  0.0 125.3 jit_solution(2711351822491708384)
XLA Ops:
  0.6 118.9 %layer.1 = (bf16[128,4096]{1,0:T(8,128)(2,1)}, bf16[8,16,4096]{2,1,0:T(8,128)(2,1)}, bf16[8,16,4096]{2,1,0:T(8,128)(2,1)}) custom-call(bf16[128,4096]{1,0:T(8,128)(2,1)} %tokens.1, bf16[4096,1792]{1,0:T(8,128)(2,1)} %gate.1, bf16[128,1792]{1,0:T(8,128)(2,1)} %up.1, bf16[1792,128]{1,0:T(8,128)(2,1)} %down.1, bf16[128,4096]{1,0:T(8,128)(2,1)} %cotangent.1, ...), custom_call_target="tpu_custom_call" | custom-call | flops 22499999744 | bytes 16000000 | tf_op jit(solution)/shard_map/layer/pallas_call | solution.py:525
  119.6 0.0 copy-start
  119.6 3.1 %fusion = f32[4096,128]{1,0:T(8,128)} fusion(bf16[128,4096]{1,0:T(8,128)(2,1)} %bitcast.8), kind=kOutput, calls=%fused_computation.2 | convolution fusion | flops 134234112 | bytes 3145728 | tf_op jit(solution)/shard_map/dot_general | solution.py:588
  122.7 0.0 copy-done
  122.7 0.0 copy-start.1
  122.7 1.6 %bitcast_convert_fusion = f32[128,4096]{1,0:T(8,128)} fusion(bf16[8,16,4096]{2,1,0:T(8,128)(2,1)S(1)} %copy-done), kind=kLoop, calls=%fused_computation | loop fusion | flops 524288 | bytes 3145728 | tf_op jit(solution)/shard_map/convert_element_type | solution.py:589
  124.3 0.0 copy-done.1
  124.3 1.0 copy.14
Async XLA Ops:
  119.6 3.1 %copy-start = (bf16[8,16,4096]{2,1,0:T(8,128)(2,1)S(1)}, bf16[8,16,4096]{2,1,0:T(8,128)(2,1)}, u32[]{:S(2)}) copy-start(bf16[8,16,4096]{2,1,0:T(8,128)(2,1)} %get-tuple-element.8) | copy-start | bytes 3145732
  122.7 1.6 %copy-start.1 = (bf16[128,4096]{1,0:T(8,128)(2,1)S(1)}, bf16[128,4096]{1,0:T(8,128)(2,1)}, u32[]{:S(2)}) copy-start(bf16[128,4096]{1,0:T(8,128)(2,1)} %get-tuple-element.12) | copy-start | bytes 3145732

commit v6 on v5

--- a/solution.py
+++ b/solution.py
@@ -476,11 +476,13 @@
     for target in targets.values():
         pl.semaphore_signal(barrier, inc=1, device_id=target, device_id_type=MESH)
     pl.semaphore_wait(barrier, len(targets))
-    for load in loads:
-        load.wait()
-    gate_waited = False
+    gate_waited = loads_waited = False
     used = []
     for what, item in order:
+        if not loads_waited and "L" in item.after:
+            for load in loads:
+                load.wait()
+            loads_waited = True
         if item.name[0] == "D" and what == "task":
             if len(used) >= SLOTS:
                 early = by_name["Q" + used[-SLOTS]]

time: 125 us -> 125 us (level)
  no operation moved by 1% of the time
where the time goes in v6:
time: 125 us
  Pallas kernels  119 us (95%)
  matrix products  3.1 us (2%)
  other arithmetic  1.6 us (1%)
    pallas_call x1, Pallas kernels, layer(): pl.pallas_call(kernel, out_shape=(jax.ShapeDtypeStruct((128, 4096), BF),...  119 us
    dot_general x1, matrix products, shards(): lax.dot_general(grads_low.reshape(128, 4096), unit, (((0,), (0,)), ((), (...  3.1 us

profile of v6, /device:TPU:0, one launch (start us, length us, event | category | flops | bytes accessed | tf_op | source)
XLA Modules:
  0.0 125.3 jit_solution(7100528331998053586)
XLA Ops:
  0.6 118.9 %layer.1 = (bf16[128,4096]{1,0:T(8,128)(2,1)}, bf16[8,16,4096]{2,1,0:T(8,128)(2,1)}, bf16[8,16,4096]{2,1,0:T(8,128)(2,1)}) custom-call(bf16[128,4096]{1,0:T(8,128)(2,1)} %tokens.1, bf16[4096,1792]{1,0:T(8,128)(2,1)} %gate.1, bf16[128,1792]{1,0:T(8,128)(2,1)} %up.1, bf16[1792,128]{1,0:T(8,128)(2,1)} %down.1, bf16[128,4096]{1,0:T(8,128)(2,1)} %cotangent.1, ...), custom_call_target="tpu_custom_call" | custom-call | flops 22499999744 | bytes 16000000 | tf_op jit(solution)/shard_map/layer/pallas_call | solution.py:527
  119.6 0.0 copy-start
  119.6 3.1 %fusion = f32[4096,128]{1,0:T(8,128)} fusion(bf16[128,4096]{1,0:T(8,128)(2,1)} %bitcast.8), kind=kOutput, calls=%fused_computation.2 | convolution fusion | flops 134234112 | bytes 3145728 | tf_op jit(solution)/shard_map/dot_general | solution.py:590
  122.7 0.0 copy-done
  122.7 0.0 copy-start.1
  122.7 1.6 %bitcast_convert_fusion = f32[128,4096]{1,0:T(8,128)} fusion(bf16[8,16,4096]{2,1,0:T(8,128)(2,1)S(1)} %copy-done), kind=kLoop, calls=%fused_computation | loop fusion | flops 524288 | bytes 3145728 | tf_op jit(solution)/shard_map/convert_element_type | solution.py:591
  124.3 0.0 copy-done.1
  124.3 1.0 copy.14
Async XLA Ops:
  119.6 3.1 %copy-start = (bf16[8,16,4096]{2,1,0:T(8,128)(2,1)S(1)}, bf16[8,16,4096]{2,1,0:T(8,128)(2,1)}, u32[]{:S(2)}) copy-start(bf16[8,16,4096]{2,1,0:T(8,128)(2,1)} %get-tuple-element.8) | copy-start | bytes 3145732
  122.7 1.6 %copy-start.1 = (bf16[128,4096]{1,0:T(8,128)(2,1)S(1)}, bf16[128,4096]{1,0:T(8,128)(2,1)}, u32[]{:S(2)}) copy-start(bf16[128,4096]{1,0:T(8,128)(2,1)} %get-tuple-element.12) | copy-start | bytes 3145732
